TPU v7x, 32 devices: a whole 2x2x4 slice. The times are simulated.
32 devices in a mesh: gx: 4 (over y, core), gy: 4 (over z), gz: 2 (over x).
Axes of the slice: x: 2, y: 2, z: 4, core: 2. Of those that a mesh axis runs over, the one named last changes fastest.
Arguments:
- residual: float32 [32, 128, 256], P('gx', 'gy', 'gz'), may hold values from -32 to 32
- direction: float32 [32, 128, 256], P('gx', 'gy', 'gz'), may hold values from -32 to 32
- diagonal: float32 [32, 128, 256], P('gx', 'gy', 'gz'), may hold values from 0.5 to 2
- recycled: bfloat16 [16, 32, 128, 256], P(None, 'gx', 'gy', 'gz'), may hold values from -6 to 6
- recycled_images: bfloat16 [16, 32, 128, 256], P(None, 'gx', 'gy', 'gz'), may hold values from -0.0014648438 to 0.0014648438
- coupling_inverse: float32 [16, 16], replicated, may hold values from -1 to 3, as said below
Outputs:
- solution_delta: float32 [32, 128, 256], P('gx', 'gy', 'gz')
- new_residual: float32 [32, 128, 256], P('gx', 'gy', 'gz')
- new_direction: float32 [32, 128, 256], P('gx', 'gy', 'gz')
Inputs may be any that keep to these rules, and one draw needn't show every extreme that they name: `coupling_inverse`: symmetric.
All inputs are finite; a program needn't handle non-finite values.
Results may differ from a plain program's by a relative error of at most 0.0028.
Values sent between devices are 32-bit elements; how exact they have to be, the bound alone decides.
No kernel may reach another device: no remote copies, remote signals or barrier semaphores. Data moves between devices by JAX's collectives and lax.ppermute only.
A program may use at most 64 MiB of HBM per device.

v0:
```python
import jax
import jax.numpy as jnp
import numpy as np
from jax import lax
from jax.experimental import pallas as pl
from jax.experimental.pallas import tpu as pltpu
from jax.sharding import PartitionSpec as P

S = 4
BASIS = 9
RECYCLED = 16
LANES = 128
TILE = 8
AXES = ("gx", "gy", "gz")

RIM = 2 * S
SIDE = RIM * S


center = 7.25
half_width = 6.75


def lanes_of(rows):
    return lax.broadcasted_iota(jnp.int32, (rows, LANES), 1)


def rows_of(rows):
    return lax.broadcasted_iota(jnp.int32, (rows, LANES), 0)


def turn(values, shift, axis):
    shift = shift % values.shape[axis]
    return pltpu.roll(values, shift, axis) if shift else values


def load_kernel(
    direction_in, residual_in, diagonal_in, coupling_in, direction, residual, diagonal, upper, lower, coupling, done
):
    pairs = (
        (direction_in, direction, S),
        (residual_in, residual, S - 1),
        (diagonal_in, diagonal, S - 1),
        (coupling_in, coupling, 0),
    )
    copies = [pltpu.make_async_copy(source, kept, done.at[index]) for index, (source, kept, _) in enumerate(pairs)]
    for copy in copies:
        copy.start()
    planes = direction.shape[0]
    at = 0
    for copy, (_, kept, width) in zip(copies, pairs):
        copy.wait()
        if not width:
            continue
        upper[at : at + width] = kept[planes - width :]
        lower[at : at + width] = kept[:width]
        at += width


def rim_kernel(direction, residual, diagonal, coupling, rim_out, after_out, before_out, coupling_out):
    planes, rows, _ = direction.shape
    slot = lanes_of(rows) // RIM
    after = jnp.zeros((rows, LANES), jnp.float32)
    before = jnp.zeros((rows, LANES), jnp.float32)
    source = lax.broadcasted_iota(jnp.int32, (LANES, LANES), 0)
    target = lax.broadcasted_iota(jnp.int32, (LANES, LANES), 1) % RIM
    ends = (source == jnp.where(target < S, target, LANES - RIM + target)).astype(jnp.float32).astype(jnp.bfloat16)
    ends = jnp.concatenate([ends, ends], axis=0)
    for field, values in enumerate((direction, residual, diagonal)):
        values = values[...].reshape(planes * rows, LANES)
        copies = jnp.dot(jnp.concatenate(split(values), axis=1), ends, preferred_element_type=jnp.float32)
        rim = jnp.zeros((rows, LANES), jnp.float32)
        for plane in range(planes):
            here = copies[rows * plane : rows * (plane + 1)]
            rim = jnp.where(slot == plane + S, here, rim)
            if plane < S:
                before = jnp.where(slot == S * field + plane, here, before)
            if plane >= planes - S:
                after = jnp.where(slot == S * field + plane - planes + S, here, after)
        rim_out[field] = rim
    after_out[...] = after
    before_out[...] = before
    vector = lax.broadcasted_iota(jnp.int32, (RECYCLED, LANES), 0)
    spread = (lanes_of(RECYCLED) // TILE == vector).astype(jnp.float32)
    coupling_out[...] = jnp.dot(
        coupling[...], spread, precision=lax.Precision.HIGHEST, preferred_element_type=jnp.float32
    )


def plane_of(own, low, high, field, x):
    planes = own.shape[0]
    first = (0, S, 2 * S - 1)[field]
    width = (S, S - 1, S - 1)[field]
    if x < 0:
        return low[first + width + x]
    if x >= planes:
        return high[first + x - planes]
    return own[x]


def packing(planes):
    pieces = []
    for field in range(3):
        reach = (S, S - 1, S - 1)[field]
        for x in range(1 - reach, planes + reach - 1):
            pieces.append((reach - max(0, -x, x - planes + 1), field, x))
        pieces.append((reach - 1, field, None))
    pieces.sort(key=lambda piece: -piece[0])
    tiles = []
    for count, field, x in pieces:
        for tile in tiles:
            used = sum(piece[0] for piece in tile)
            if used + count <= TILE:
                tile.append((count, field, x, used))
                break
        else:
            tiles.append([(count, field, x, 0)])
    return tiles


def edge_kernel(
    parity, direction, residual, diagonal, low, high, rim_next, rim_before, rim_low_next, rim_low_before, rim_high_next, rim_high_before, first_out, second_out, rim_out
):
    planes, rows, _ = direction.shape
    lane = lanes_of(rows)
    nearer = lane % RIM < S
    low_rim = jnp.where(nearer, rim_low_next[...], rim_low_before[...])
    high_rim = jnp.where(nearer, rim_high_next[...], rim_high_before[...])
    for field in range(3):
        rim = jnp.where(nearer, rim_next[field], rim_before[field])
        rim = jnp.where(lane < SIDE, turn(low_rim, -SIDE * field, 1), rim)
        rim = jnp.where(lane >= SIDE + RIM * planes, turn(high_rim, SIDE + RIM * planes - SIDE * field, 1), rim)
        rim_out[field] = rim
    fields = (direction, residual, diagonal)
    row = rows_of(TILE)

    even = parity[0] == 0
    for index, tile in enumerate(packing(planes)):
        lower = jnp.zeros((TILE, LANES), jnp.float32)
        upper = jnp.zeros((TILE, LANES), jnp.float32)
        for count, field, x, offset in tile:
            values = rim_out[field] if x is None else plane_of(fields[field], low, high, field, x)
            mine = (row >= offset) & (row < offset + count)
            lower = jnp.where(mine, turn(values[:TILE], offset, 0), lower)
            upper = jnp.where(mine, turn(values[rows - TILE :], offset + count, 0), upper)
        first_out[index] = jnp.where(even, upper, lower)
        second_out[index] = jnp.where(even, lower, upper)


def shift_matrices():
    source = np.arange(LANES)[:, None]
    target = np.arange(LANES)[None, :]
    along = np.abs(source - target) == 1
    last = (target % RIM == 0) & (source == LANES - 1)
    ends = last | ((target % RIM == RIM - 1) & (source == 0))
    facing = ((target == 0) & (source % RIM == RIM - 1)) | ((target == LANES - 1) & (source % RIM == 0))
    around = (np.abs(source - target) == RIM) | (along & (source // RIM == target // RIM))
    groups = np.arange(2 * TILE * RECYCLED)[:, None] // (2 * TILE) == target // TILE
    inner = np.concatenate([along, ends], 1)
    outer = np.concatenate([facing, np.zeros_like(facing)], 1)
    matrices = ([inner, inner, outer, outer], [around, around], [groups, groups, groups])
    return [jnp.asarray(np.concatenate(parts), jnp.bfloat16) for parts in matrices]


def split(values, count=2):
    terms = []
    for index in range(count):
        terms.append(values.astype(jnp.bfloat16))
        if index + 1 < count:
            values = values - terms[-1].astype(jnp.float32)
    return terms


def products():
    found = []
    for one, other, count in ((0, 0, 2 * S + 1), (S + 1, S + 1, 2 * S - 1), (0, S + 1, 2 * S)):
        found.append([(one + (m + 1) // 2, other + m // 2) for m in range(count)])
    return found


def march(load, vertical, planes, ring, walk, trail, weight, left, shifts, rim_shifts, emit, keep):
    slot = lanes_of(ring) // RIM

    def scaled(values):
        return (values - (center - 6.0)) * (2.0 / half_width)

    for x in range(1 - S, planes + S - 1):
        weight[x + S] = scaled(load(2, x))
    weight_rim = scaled(load(2, None))
    chains = ((0, walk, 0, S), (1, trail, S, S - 1))
    rim_levels = {}
    for field, history, offset, length in chains:
        for x in range(-length, planes + length):
            history[0, x + S] = load(field, x)
        rim_levels[field] = [load(field, None)]
        keep(field, 0, rim_levels[field][0])

    def advance(values, before, factor, beside):
        following = factor * values - (2.0 / half_width) * beside
        return 0.5 * following if before is None else following - before

    for level in range(S):
        work = []
        for field, history, offset, length in chains:
            reach = length - 1 - level
            if reach < 0:
                continue
            facing = [part.astype(jnp.float32) for part in split(rim_levels[field][level])]
            for x in range(-reach, planes + reach):
                parts = list(split(history[level, x + S]))
                parts += [jnp.where(slot == x + S, part, 0.0).astype(jnp.bfloat16) for part in facing]
                for index, part in enumerate(parts):
                    left[ring * len(work) : ring * (len(work) + 1), LANES * index : LANES * (index + 1)] = part
                work.append((field, history, offset, reach, x))
        moved = jnp.dot(left[: ring * len(work)], shifts[...], preferred_element_type=jnp.float32)
        gathered = {}
        for index, (field, history, offset, reach, x) in enumerate(work):
            at = x + S
            here = moved[ring * index : ring * (index + 1)]
            values = history[level, at]
            beside = here[:, :LANES] + (history[level, at - 1] + history[level, at + 1])
            beside = beside + vertical(values, field, level, x)
            before = None if level == 0 else history[level - 1, at]
            following = advance(values, before, weight[at], beside)
            if 0 <= x < planes:
                emit(offset + level, x, following)
            if reach:
                history[level + 1, at] = following
                gathered[field] = jnp.where(slot == at, here[:, LANES:], gathered.get(field, 0.0))
        for field in gathered:
            levels = rim_levels[field]
            rim = levels[level]
            beside = jnp.dot(
                jnp.concatenate(split(rim), axis=1), rim_shifts[...], preferred_element_type=jnp.float32
            )
            beside = beside + vertical(rim, field, level, None) + gathered[field]
            levels.append(advance(rim, None if level == 0 else levels[level - 1], weight_rim, beside))
            keep(field, level + 1, levels[-1])


def inner_products(planes, tiles_of, images_of):
    families = products()
    sums = {}
    half = 2 * TILE
    total = jnp.zeros((BASIS * half, RECYCLED * half), jnp.float32)
    rounded = []
    against = []
    for x in range(planes):
        values = [tiles_of(index, x) for index in range(BASIS)]
        for tile in range(len(values[0])):
            if values[0][tile] is None:
                continue
            for family in families:
                for i, j in family:
                    product = values[i][tile] * values[j][tile]
                    sums[i, j] = sums[i, j] + product if (i, j) in sums else product
        nothing = jnp.zeros((TILE, LANES), jnp.float32)
        for block, images in enumerate(images_of(x)):
            pieces = [value[2 * block : 2 * block + 2] for value in values]
            pieces = [nothing if piece is None else piece for pair in pieces for piece in pair]
            rounded.append(jnp.concatenate(pieces, axis=0).astype(jnp.bfloat16))
            against.append(images.reshape(RECYCLED * half, LANES))
        if len(rounded) == 2:
            total = total + lax.dot_general(
                jnp.concatenate(rounded, axis=1),
                jnp.concatenate(against, axis=1),
                (((1,), (1,)), ((), ())),
                preferred_element_type=jnp.float32,
            )
            rounded = []
            against = []
    return sums, total


def inner_kernel(
    direction, residual, diagonal, low, high, rims, shifts, rim_shifts, images_in, basis_out, sums_out, total_out, walk, trail, rim_walk, rim_trail, images, weight, left, done
):
    planes, rows, _ = direction.shape
    fields = (direction, residual, diagonal)
    row = rows_of(TILE)
    copy = pltpu.make_async_copy(images_in, images, done)
    copy.start()

    def load(field, x):
        return rims[field] if x is None else plane_of(fields[field], low, high, field, x)

    def vertical(values, field, level, x):
        return turn(values, 1, 0) + turn(values, -1, 0)

    def emit(index, x, values):
        basis_out[index, x] = values

    def keep(field, level, values):
        (rim_trail if field else rim_walk)[level] = values

    march(load, vertical, planes, rows, walk, trail, weight, left, shifts, rim_shifts, emit, keep)

    def tiles_of(index, x):
        if index in (0, S + 1):
            values = fields[index > 0][x]
        else:
            values = basis_out[index - 1 if index <= S else index - 2, x]
        tiles = [values[start : start + TILE] for start in range(0, rows, TILE)]
        tiles[0] = jnp.where(row < S, 0.0, tiles[0])
        tiles[-1] = jnp.where(row < S, tiles[-1], 0.0)
        return tiles

    copy.wait()

    def images_of(x):
        return [images[:, x, start : start + 2 * TILE] for start in range(0, rows, 2 * TILE)]

    sums, total = inner_products(planes, tiles_of, images_of)
    for index, pair in enumerate(sorted(sums)):
        sums_out[index] = sums[pair]
    total_out[...] = total


def caps_kernel(
    parity, direction, residual, diagonal, low, high, rims, first, second, images, shifts, rim_shifts, groups, sums_in, total_in, inner_walk, inner_trail, inner_rim_walk, inner_rim_trail, caps_out, parts_out, walk, trail, weight, left
):
    planes, rows, _ = direction.shape
    ring = 2 * TILE
    fields = (direction, residual, diagonal)
    row = rows_of(TILE)
    near = row < S
    even = parity[0] == 0
    halo = {}
    for index, tile in enumerate(packing(planes)):
        above = jnp.where(even, first[index], second[index])
        below = jnp.where(even, second[index], first[index])
        for count, field, x, offset in tile:
            halo[field, x] = jnp.where(near, turn(above, -offset, 0), turn(below, -offset - count, 0))
    nothing = jnp.zeros((TILE, LANES), jnp.float32)

    def load(field, x):
        values = rims[field] if x is None else plane_of(fields[field], low, high, field, x)
        beyond = halo.get((field, x), nothing)
        return jnp.concatenate(
            [jnp.where(near, beyond, values[rows - TILE :]), jnp.where(near, values[:TILE], beyond)], axis=0
        )

    def vertical(values, field, level, x):
        if x is None:
            known = (inner_rim_trail if field else inner_rim_walk)[level]
        else:
            known = (inner_trail if field else inner_walk)[level, x + S]
        top = values[:TILE]
        bottom = values[TILE:]
        top_sum = turn(top, -1, 0) + turn(jnp.where(row == S - 1, known[rows - TILE :], top), 1, 0)
        bottom_sum = turn(jnp.where(row == S, known[:TILE], bottom), -1, 0) + turn(bottom, 1, 0)
        return jnp.concatenate([top_sum, bottom_sum], axis=0)

    def emit(index, x, values):
        caps_out[index, x] = jnp.where(near, values[TILE:], values[:TILE])

    march(load, vertical, planes, ring, walk, trail, weight, left, shifts, rim_shifts, emit, lambda *_: None)

    def tile_of(index, x):
        if index in (0, S + 1):
            values = fields[index > 0][x]
            return jnp.where(near, values[:TILE], values[rows - TILE :])
        return caps_out[index - 1 if index <= S else index - 2, x]

    upper = lax.broadcasted_iota(jnp.int32, (RECYCLED, 2 * TILE, LANES), 1) < TILE
    families = products()
    sums = {}
    half = 2 * TILE
    total = total_in[...]
    for x in range(0, planes, 2):
        rounded = []
        against = []
        for k in range(2):
            values = [tile_of(index, x + k) for index in range(BASIS)]
            for family in families:
                for i, j in family:
                    product = values[i] * values[j]
                    sums[i, j] = sums[i, j] + product if (i, j) in sums else product
            pieces = [
                piece for value in values for piece in (jnp.where(near, value, 0.0), jnp.where(near, 0.0, value))
            ]
            rounded.append(jnp.concatenate(pieces, axis=0).astype(jnp.bfloat16))
            images_here = jnp.where(upper, images[:, x + k, :half], images[:, x + k, rows - half :])
            against.append(images_here.reshape(RECYCLED * half, LANES))
        total = total + lax.dot_general(
            jnp.concatenate(rounded, axis=1),
            jnp.concatenate(against, axis=1),
            (((1,), (1,)), ((), ())),
            preferred_element_type=jnp.float32,
        )
    spot = lanes_of(TILE)
    columns = [list(families[0][:TILE]), list(families[1]) + [families[0][TILE]], list(families[2])]
    order = {pair: index for index, pair in enumerate(sorted(sums))}
    scalars = jnp.zeros((TILE, LANES), jnp.float32)
    for place, column in enumerate(columns):
        values = jnp.zeros((TILE, LANES), jnp.float32)
        for index, pair in enumerate(column):
            whole = sums[pair] + sums_in[order[pair]]
            values = jnp.where(row == index, jnp.sum(whole, axis=0, keepdims=True), values)
        values = jnp.sum(values, axis=1, keepdims=True)
        scalars = jnp.where((spot // TILE == row) & (spot % TILE == place + 1), values, scalars)
    wide = (BASIS * half, RECYCLED * half)
    same = lax.broadcasted_iota(jnp.int32, wide, 0) % half == lax.broadcasted_iota(jnp.int32, wide, 1) % half
    total = jnp.where(same, total, 0.0).reshape(BASIS, 2, TILE, RECYCLED * half)
    total = (total[:, 0] + total[:, 1]).reshape(BASIS * TILE, RECYCLED * half)
    lines = jnp.dot(jnp.concatenate(split(total, 3), axis=1), groups[...], preferred_element_type=jnp.float32)
    mixed = jnp.zeros((TILE, LANES), jnp.float32)
    for index in range(TILE):
        mixed = jnp.where(spot % TILE == index, lines[TILE * index : TILE * (index + 1)], mixed)
    extra = jnp.where(spot % TILE == 0, lines[TILE * TILE :], scalars)
    table = jnp.concatenate(
        [jnp.sum(mixed, axis=0, keepdims=True), jnp.sum(extra, axis=0, keepdims=True)], axis=0
    )
    for device in range(parts_out.shape[0]):
        parts_out[device] = table


def moments_of(values):
    first = values[:2]
    return first + [2.0 * value - first[index % 2] for index, value in enumerate(values[2:])]


def finish_kernel(
    parts, coupling, direction, residual, basis, caps, recycled, delta_out, residual_out, direction_out
):
    table = jnp.sum(parts[...], axis=0)
    spot = lanes_of(TILE)
    row = rows_of(TILE)
    mixed = jnp.broadcast_to(table[:1], (TILE, LANES))
    extra = jnp.broadcast_to(table[1:], (TILE, LANES))
    columns = []
    for place in range(3):
        mine = (spot // TILE == row) & (spot % TILE == place + 1)
        column = jnp.sum(jnp.where(mine, extra, 0.0), axis=1, keepdims=True)
        columns.append(jnp.broadcast_to(column, (TILE, LANES)))

    def spread(column, index):
        return jnp.broadcast_to(columns[column][index : index + 1], (TILE, LANES))

    walk = moments_of([spread(0, index) for index in range(TILE)] + [spread(1, TILE - 1)])
    trail = moments_of([spread(1, index) for index in range(2 * S - 1)])
    cross = moments_of([spread(2, index) for index in range(2 * S)])
    gram = {}
    for i in range(BASIS):
        for j in range(i, BASIS):
            source = walk if j <= S else (cross if i <= S else trail)
            one = i if i <= S else i - S - 1
            two = j if j <= S else j - S - 1
            gram[i, j] = gram[j, i] = 0.5 * (source[one + two] + source[abs(one - two)])

    def dot(one, other):
        terms = [one[i] * other[i] for i in one if i in other]
        while len(terms) > 1:
            terms = [a + b for a, b in zip(terms[::2], terms[1::2])] + terms[len(terms) // 2 * 2 :]
        return terms[0]

    def applied(values):
        return {i: dot({j: gram[i, j] for j in values}, values) for i in range(BASIS)}

    def mapped_by(values):
        found = {}
        for j, value in values.items():
            first, length = (0, S + 1) if j <= S else (S + 1, S)
            k = j - first
            if k == 0:
                entries = ((j, center), (j + 1, half_width))
            elif k < length - 1:
                entries = ((j - 1, half_width / 2), (j, center), (j + 1, half_width / 2))
            else:
                entries = ()
            for i, factor in entries:
                found[i] = found[i] + factor * value if i in found else factor * value
        return found

    def plus(one, factor, other):
        found = dict(one)
        for i, value in other.items():
            found[i] = found[i] + factor * value if i in found else factor * value
        return found

    unit = jnp.ones((TILE, LANES), jnp.float32)
    residue = {S + 1: unit}
    search = {0: unit}
    update = {}
    norm_now = dot(residue, applied(residue))
    for _ in range(S):
        mapped = mapped_by(search)
        step_size = norm_now / dot(search, applied(mapped))
        update = plus(update, step_size, search)
        residue = plus(residue, -step_size, mapped)
        norm_next = dot(residue, applied(residue))
        search = plus(residue, norm_next / norm_now, search)
        norm_now = norm_next
    across = residue[0]
    for index in range(1, TILE):
        across = jnp.where(spot % TILE == index, residue[index], across)
    projected = mixed * across + jnp.where(spot % TILE == 0, extra * residue[BASIS - 1], 0.0)
    projected = projected[:1]
    weights = jnp.sum(coupling[...] * projected, axis=1, keepdims=True)
    weights = jnp.broadcast_to(weights.astype(jnp.bfloat16).astype(jnp.float32), (RECYCLED, LANES))
    planes, rows, _ = direction.shape
    near = row < S
    for plane in range(planes):
        for start in range(0, rows, 2 * TILE):
            part = slice(start, start + 2 * TILE)
            found = [0.0, 0.0, 0.0]
            for field in range(BASIS):
                if field in (0, S + 1):
                    values = (residual if field else direction)[plane, part]
                else:
                    at = field - 1 if field <= S else field - 2
                    pieces = [basis[at, plane, start : start + TILE], basis[at, plane, start + TILE : start + 2 * TILE]]
                    if start == 0:
                        pieces[0] = jnp.where(near, caps[at, plane], pieces[0])
                    if start + 2 * TILE == rows:
                        pieces[1] = jnp.where(near, pieces[1], caps[at, plane])
                    values = jnp.concatenate(pieces, axis=0)
                for index, coefficients in enumerate((update, residue, search)):
                    if field in coefficients:
                        factor = jnp.concatenate([coefficients[field]] * 2, axis=0)
                        found[index] = found[index] + factor * values
            correction = 0.0
            for vector in range(RECYCLED):
                correction = correction + weights[vector : vector + 1] * recycled[vector, plane, part].astype(
                    jnp.float32
                )
            delta_out[plane, part] = found[0]
            residual_out[plane, part] = found[1]
            direction_out[plane, part] = found[2] - correction


def shifted(values, shifts):
    axes = tuple(shifts)
    counts = [lax.axis_size(axis) for axis in axes]
    pairs = [(0, 0)]
    for axis, count in zip(axes, counts):
        pairs = [
            (source * count + i, target * count + (i + shifts[axis]) % count)
            for source, target in pairs
            for i in range(count)
        ]
    return lax.ppermute(values, axes, pairs)


def call(kernel, out_shape, operands, scratch=(), limit=16, in_hbm=()):
    in_vmem = pl.BlockSpec(memory_space=pltpu.VMEM)
    in_smem = pl.BlockSpec(memory_space=pltpu.SMEM)
    in_place = pl.BlockSpec(memory_space=pltpu.HBM)
    in_hbm = [pltpu.with_memory_space_constraint(operand, pltpu.HBM) for operand in in_hbm]
    out_shape = [shape if isinstance(shape, jax.ShapeDtypeStruct) else jax.ShapeDtypeStruct(shape, jnp.float32) for shape in out_shape]
    return pl.pallas_call(
        kernel,
        out_shape=tuple(out_shape),
        in_specs=[in_smem if operand.dtype == jnp.int32 else in_vmem for operand in operands] + [in_place] * len(in_hbm),
        out_specs=(in_vmem,) * len(out_shape),
        scratch_shapes=list(scratch),
        compiler_params=pltpu.CompilerParams(vmem_limit_bytes=limit * 1024 * 1024),
    )(*operands, *in_hbm)


def body(residual, direction, diagonal, recycled, recycled_images, coupling_inverse):
    planes, rows, columns = residual.shape
    if columns != LANES or rows != 4 * TILE or RIM * (planes + 2 * S) != LANES or lax.axis_size("gy") % 2:
        raise ValueError("unsupported block")
    shape = residual.shape
    shifts, rim_shifts, groups = shift_matrices()
    slab = (3 * S - 2, rows, LANES)
    *fields, upper, lower, coupling = call(
        load_kernel,
        [shape] * 3 + [slab] * 2 + [coupling_inverse.shape],
        (),
        [pltpu.SemaphoreType.DMA((4,))],
        in_hbm=(direction, residual, diagonal, coupling_inverse),
    )
    low = shifted(upper, {"gx": 1})
    high = shifted(lower, {"gx": -1})
    rim, rim_after, rim_before, coupling = call(
        rim_kernel, [(3, rows, LANES), (rows, LANES), (rows, LANES), (RECYCLED, LANES)], (*fields, coupling)
    )
    sides = (-1,) if lax.axis_size("gz") == 2 else (-1, 1)
    rims = [shifted(rim, {"gz": side}) for side in sides]
    low_rims = [shifted(rim_after, {"gx": 1, "gz": side}) for side in sides]
    high_rims = [shifted(rim_before, {"gx": -1, "gz": side}) for side in sides]
    parity = (lax.axis_index("gy") & 1).astype(jnp.int32).reshape(1)
    tiles = len(packing(planes))
    first, second, whole_rims = call(
        edge_kernel,
        [(tiles, TILE, LANES), (tiles, TILE, LANES), (3, rows, LANES)],
        (parity, *fields, low, high, rims[0], rims[-1], low_rims[0], low_rims[-1], high_rims[0], high_rims[-1]),
    )
    count = lax.axis_size("gy")
    second = lax.ppermute(second, "gy", [(i, (i - 1 + 2 * (i % 2)) % count) for i in range(count)])
    first = lax.ppermute(first, "gy", [(i, i ^ 1) for i in range(count)])
    devices = lax.axis_size(AXES)
    wide = planes + 2 * S
    worked = 2 * planes + 2 * (S - 1) + 2 * (S - 2)

    def weights_and_left(ring):
        return [pltpu.VMEM((wide, ring, LANES), jnp.float32), pltpu.VMEM((worked * ring, 4 * LANES), jnp.bfloat16)]

    count = sum(len(family) for family in products())
    block = 2 * TILE
    basis, sums, total, *levels, images = call(
        inner_kernel,
        [
            (BASIS - 2, *shape),
            (count, TILE, LANES),
            (BASIS * block, RECYCLED * block),
            (S, wide, rows, LANES),
            (S - 1, wide, rows, LANES),
            (S, rows, LANES),
            (S - 1, rows, LANES),
            jax.ShapeDtypeStruct(recycled_images.shape, recycled_images.dtype),
        ],
        (*fields, low, high, whole_rims, shifts, rim_shifts),
        weights_and_left(rows) + [pltpu.SemaphoreType.DMA],
        in_hbm=(recycled_images,),
    )
    caps, parts = call(
        caps_kernel,
        [(BASIS - 2, planes, TILE, LANES), (devices, 2, LANES)],
        (parity, *fields, low, high, whole_rims, first, second, images)
        + (shifts, rim_shifts, groups, sums, total, *levels),
        [pltpu.VMEM((S, wide, block, LANES), jnp.float32), pltpu.VMEM((S - 1, wide, block, LANES), jnp.float32)]
        + weights_and_left(block),
    )
    parts = lax.all_to_all(parts, AXES, 0, 0)
    return call(finish_kernel, [shape] * 3, (parts, coupling, fields[0], fields[1], basis, caps, recycled))


def solution(mesh):
    in_specs = (
        P("gx", "gy", "gz"),
        P("gx", "gy", "gz"),
        P("gx", "gy", "gz"),
        P(None, "gx", "gy", "gz"),
        P(None, "gx", "gy", "gz"),
        P(),
    )
    out_specs = (P("gx", "gy", "gz"), P("gx", "gy", "gz"), P("gx", "gy", "gz"))
    return jax.shard_map(body, mesh=mesh, in_specs=in_specs, out_specs=out_specs, check_vma=False)
```

profile of v0, /device:TPU:0, one launch (start us, length us, event | category | flops | bytes accessed | tf_op | source)
XLA Modules:
  0.0 32.7 jit_solution(5002873699771489514)
XLA Ops:
  0.6 1.1 %shard_map.112 = (f32[8,32,128]{2,1,0:T(8,128)S(1)}, f32[8,32,128]{2,1,0:T(8,128)S(1)}, f32[8,32,128]{2,1,0:T(8,128)S(1)}, f32[10,32,128]{2,1,0:T(8,128)S(1)}, f...) custom-call(f32[8,32,128]{2,1,0:T(8,128)} %direction_in.1, f32[8,32,128]{2,1,0:T(8,128)} %residual_in.1, ...), custom_call_target="tpu_custom_call" | custom-call | tf_op jit(solution)/shard_map/pallas_call | solution.py:551
  1.7 0.5 %collective-permute-start = (f32[10,32,128]{2,1,0:T(8,128)S(1)}, f32[10,32,128]{2,1,0:T(8,128)S(1)}, u32[]{:S(2)}, u32[]{:S(2)}) collective-permute-start(f32[10,32,128]{2,1,0:T(8,128)S(1)} %get-tuple-element.29), channel_id=1, source_target_pairs={{0,8},{8,16},{16,24},{24,0},{1,9},{9,17},{17,25},{25,1},{2,10},{10... | collective-permute-start | bytes 491528 | tf_op jit(solution)/shard_map/ppermute | solution.py:542
  2.3 2.0 %collective-permute-start.1 = (f32[10,32,128]{2,1,0:T(8,128)S(1)}, f32[10,32,128]{2,1,0:T(8,128)S(1)}, u32[]{:S(2)}, u32[]{:S(2)}) collective-permute-start(f32[10,32,128]{2,1,0:T(8,128)S(1)} %get-tuple-element.30), channel_id=1, source_target_pairs={{0,24},{8,0},{16,8},{24,16},{1,25},{9,1},{17,9},{25,17},{2,26},{10... | collective-permute-start | bytes 491528 | tf_op jit(solution)/shard_map/ppermute | solution.py:542
  4.3 0.3 shard_map.113
  4.5 2.3 %collective-permute-start.2 = (f32[3,32,128]{2,1,0:T(8,128)S(1)}, f32[3,32,128]{2,1,0:T(8,128)S(1)}, u32[]{:S(2)}, u32[]{:S(2)}) collective-permute-start(f32[3,32,128]{2,1,0:T(8,128)S(1)} %get-tuple-element.32), channel_id=1, source_target_pairs={{0,1},{1,0},{2,3},{3,2},{4,5},{5,4},{6,7},{7,6},{8,9},{9,8},{10,11... | collective-permute-start | bytes 147464 | tf_op jit(solution)/shard_map/ppermute | solution.py:542
  6.8 0.0 collective-permute-start.3
  6.8 2.6 %collective-permute-start.4 = (f32[32,128]{1,0:T(8,128)S(1)}, f32[32,128]{1,0:T(8,128)S(1)}, u32[]{:S(2)}, u32[]{:S(2)}) collective-permute-start(f32[32,128]{1,0:T(8,128)S(1)} %get-tuple-element.34), channel_id=1, source_target_pairs={{0,25},{1,24},{8,1},{9,0},{16,9},{17,8},{24,17},{25,16},{2,27},{3,... | collective-permute-start | bytes 49160 | tf_op jit(solution)/shard_map/ppermute | solution.py:542
  9.5 1.4 %collective-permute-done.3.rim_low_next.rim_low_before = f32[32,128]{1,0:T(8,128)S(1)} collective-permute-done((f32[32,128]{1,0:T(8,128)S(1)}, f32[32,128]{1,0:T(8,128)S(1)}, u32[]{:S(2)}, u32[]{:S(2)}) %collective-permute-start.3) | collective-permute-done | bytes 16416 | tf_op jit(solution)/shard_map/ppermute | solution.py:542
  10.9 0.3 collective-permute-done.4.rim_high_next.rim_high_before
  11.2 0.0 collective-permute-done.2.rim_next.rim_before
  11.2 0.0 collective-permute-done.low
  11.2 0.0 collective-permute-done.1.high
  11.2 0.0 copy-start.1
  11.2 0.0 copy-start.2
  11.2 0.1 shard_map.114
  11.3 1.6 %collective-permute-start.5 = (f32[14,8,128]{2,1,0:T(8,128)S(1)}, f32[14,8,128]{2,1,0:T(8,128)S(1)}, u32[]{:S(2)}, u32[]{:S(2)}) collective-permute-start(f32[14,8,128]{2,1,0:T(8,128)S(1)} %get-tuple-element.36), channel_id=1, source_target_pairs={{0,2},{2,0},{4,6},{6,4},{1,3},{3,1},{5,7},{7,5},{8,10},{10,8},{12,... | collective-permute-start | bytes 172040 | tf_op jit(solution)/shard_map/ppermute | solution.py:593
  12.9 2.5 %collective-permute-start.6 = (f32[14,8,128]{2,1,0:T(8,128)S(1)}, f32[14,8,128]{2,1,0:T(8,128)S(1)}, u32[]{:S(2)}, u32[]{:S(2)}) collective-permute-start(f32[14,8,128]{2,1,0:T(8,128)S(1)} %get-tuple-element.37), channel_id=1, source_target_pairs={{0,6},{2,4},{4,2},{6,0},{1,7},{3,5},{5,3},{7,1},{8,14},{10,12},{12... | collective-permute-start | bytes 172040 | tf_op jit(solution)/shard_map/ppermute | solution.py:592
  15.4 0.0 copy-done.1
  15.4 0.0 copy-done.2
  15.4 0.0 copy-start.3
  15.4 2.9 %shard_map.115 = (f32[7,8,32,128]{3,2,1,0:T(8,128)S(1)}, f32[24,8,128]{2,1,0:T(8,128)S(1)}, f32[144,256]{1,0:T(8,128)S(1)}, f32[4,16,32,128]{3,2,1,0:T(8,128)S(1...) custom-call(f32[8,32,128]{2,1,0:T(8,128)S(1)} %get-tuple-element.26., ...), custom_call_target="tpu_custom_call" | custom-call | tf_op jit(solution)/shard_map/pallas_call | solution.py:551
  18.3 0.0 collective-permute-done.5.first
  18.3 1.0 %collective-permute-done.6.second = f32[14,8,128]{2,1,0:T(8,128)S(1)} collective-permute-done((f32[14,8,128]{2,1,0:T(8,128)S(1)}, f32[14,8,128]{2,1,0:T(8,128)S(1)}, u32[]{:S(2)}, u32[]{:S(2)}) %collective-permute-start.6) | collective-permute-done | bytes 57376 | tf_op jit(solution)/shard_map/ppermute | solution.py:592
  19.4 0.0 copy-done.3
  19.4 0.0 copy-start
  19.4 1.4 %shard_map.116 = (f32[7,8,8,128]{3,2,1,0:T(8,128)S(1)}, f32[32,2,128]{2,1,0:T(2,128)S(1)}) custom-call(s32[1]{0:T(128)} %bitcast.parity, f32[8,32,128]{2,1,0:T(8,128)S(1)} %get-tuple-element.26.direction, f32[8,32,128]{2,1,0:T(8,128)S(1)} %get-tuple-element.27.residual, f32[8,32,128]{2,1,0:T(8,128)S(1)} %get-tuple-element.28.diagonal, ...), custom_call_target="tpu_custom_call" | custom-call | tf_op jit(solution)/shard_map/pallas_call | solution.py:551
  20.8 10.5 %all_to_all.5.parts = f32[32,2,128]{2,1,0:T(2,128)S(1)} all-to-all(f32[32,2,128]{2,1,0:T(2,128)S(1)} %get-tuple-element.45), channel_id=1, replica_groups=mesh['gx'=4,'gy'=4,'gz'=2] {'gx','gy','gz'}, dimensions={0} | all-to-all | bytes 65536 | tf_op jit(solution)/shard_map/all_to_all | solution.py:627
  31.3 0.0 copy-done
  31.3 1.4 %shard_map.117 = (f32[8,32,128]{2,1,0:T(8,128)}, f32[8,32,128]{2,1,0:T(8,128)}, f32[8,32,128]{2,1,0:T(8,128)}) custom-call(f32[32,2,128]{2,1,0:T(2,128)S(1)} %all_to_all.5.parts, f32[16,128]{1,0:T(8,128)S(1)} %get-tuple-element.46.coupling, f32[8,32,128]{2,1,0:T(8,128)S(1)} %get-tuple-element.26.direction, f32[8,32,128]{2,1,0:T(8,128)S(1)} %get-tuple-element.27.residual, ...), custom_call_target="tpu_custom_call" | custom-call | tf_op jit(solution)/shard_map/pallas_call | solution.py:551
Async XLA Ops:
  1.7 9.5 %collective-permute-start = (f32[10,32,128]{2,1,0:T(8,128)S(1)}, f32[10,32,128]{2,1,0:T(8,128)S(1)}, u32[]{:S(2)}, u32[]{:S(2)}) collective-permute-start(f32[10,32,128]{2,1,0:T(8,128)S(1)} %get-tuple-element.29), channel_id=1, source_target_pairs={{0,8},{8,16},{16,24},{24,0},{1,9},{9,17},{17,25},{25,1},{2,10},{10... | collective-permute-start | bytes 491528 | tf_op jit(solution)/shard_map/ppermute | solution.py:542
  2.3 8.9 %collective-permute-start.1 = (f32[10,32,128]{2,1,0:T(8,128)S(1)}, f32[10,32,128]{2,1,0:T(8,128)S(1)}, u32[]{:S(2)}, u32[]{:S(2)}) collective-permute-start(f32[10,32,128]{2,1,0:T(8,128)S(1)} %get-tuple-element.30), channel_id=1, source_target_pairs={{0,24},{8,0},{16,8},{24,16},{1,25},{9,1},{17,9},{25,17},{2,26},{10... | collective-permute-start | bytes 491528 | tf_op jit(solution)/shard_map/ppermute | solution.py:542
  4.5 6.6 %collective-permute-start.2 = (f32[3,32,128]{2,1,0:T(8,128)S(1)}, f32[3,32,128]{2,1,0:T(8,128)S(1)}, u32[]{:S(2)}, u32[]{:S(2)}) collective-permute-start(f32[3,32,128]{2,1,0:T(8,128)S(1)} %get-tuple-element.32), channel_id=1, source_target_pairs={{0,1},{1,0},{2,3},{3,2},{4,5},{5,4},{6,7},{7,6},{8,9},{9,8},{10,11... | collective-permute-start | bytes 147464 | tf_op jit(solution)/shard_map/ppermute | solution.py:542
  6.8 4.1 %collective-permute-start.3 = (f32[32,128]{1,0:T(8,128)S(1)}, f32[32,128]{1,0:T(8,128)S(1)}, u32[]{:S(2)}, u32[]{:S(2)}) collective-permute-start(f32[32,128]{1,0:T(8,128)S(1)} %get-tuple-element.33), channel_id=1, source_target_pairs={{0,9},{1,8},{8,17},{9,16},{16,25},{17,24},{24,1},{25,0},{2,11},{3,... | collective-permute-start | bytes 49160 | tf_op jit(solution)/shard_map/ppermute | solution.py:542
  6.8 4.3 %collective-permute-start.4 = (f32[32,128]{1,0:T(8,128)S(1)}, f32[32,128]{1,0:T(8,128)S(1)}, u32[]{:S(2)}, u32[]{:S(2)}) collective-permute-start(f32[32,128]{1,0:T(8,128)S(1)} %get-tuple-element.34), channel_id=1, source_target_pairs={{0,25},{1,24},{8,1},{9,0},{16,9},{17,8},{24,17},{25,16},{2,27},{3,... | collective-permute-start | bytes 49160 | tf_op jit(solution)/shard_map/ppermute | solution.py:542
  11.2 4.2 %copy-start.1 = (bf16[512,256]{1,0:T(8,128)(2,1)S(1)}, bf16[512,256]{1,0:T(8,128)(2,1)}, u32[]{:S(2)}) copy-start(bf16[512,256]{1,0:T(8,128)(2,1)} %constant.14.clone.shifts) | copy-start | bytes 786436
  11.2 4.2 %copy-start.2 = (bf16[256,128]{1,0:T(8,128)(2,1)S(1)}, bf16[256,128]{1,0:T(8,128)(2,1)}, u32[]{:S(2)}) copy-start(bf16[256,128]{1,0:T(8,128)(2,1)} %constant.15.clone.rim_shifts) | copy-start | bytes 196612
  11.3 7.0 %collective-permute-start.5 = (f32[14,8,128]{2,1,0:T(8,128)S(1)}, f32[14,8,128]{2,1,0:T(8,128)S(1)}, u32[]{:S(2)}, u32[]{:S(2)}) collective-permute-start(f32[14,8,128]{2,1,0:T(8,128)S(1)} %get-tuple-element.36), channel_id=1, source_target_pairs={{0,2},{2,0},{4,6},{6,4},{1,3},{3,1},{5,7},{7,5},{8,10},{10,8},{12,... | collective-permute-start | bytes 172040 | tf_op jit(solution)/shard_map/ppermute | solution.py:593
  12.9 6.5 %collective-permute-start.6 = (f32[14,8,128]{2,1,0:T(8,128)S(1)}, f32[14,8,128]{2,1,0:T(8,128)S(1)}, u32[]{:S(2)}, u32[]{:S(2)}) collective-permute-start(f32[14,8,128]{2,1,0:T(8,128)S(1)} %get-tuple-element.37), channel_id=1, source_target_pairs={{0,6},{2,4},{4,2},{6,0},{1,7},{3,5},{5,3},{7,1},{8,14},{10,12},{12... | collective-permute-start | bytes 172040 | tf_op jit(solution)/shard_map/ppermute | solution.py:592
  15.4 4.0 %copy-start.3 = (bf16[768,128]{1,0:T(8,128)(2,1)S(1)}, bf16[768,128]{1,0:T(8,128)(2,1)}, u32[]{:S(2)}) copy-start(bf16[768,128]{1,0:T(8,128)(2,1)} %constant.16.clone.groups) | copy-start | bytes 589828
  19.4 11.9 %copy-start = (bf16[16,8,32,128]{3,2,1,0:T(8,128)(2,1)S(1)}, bf16[16,8,32,128]{3,2,1,0:T(8,128)(2,1)}, u32[]{:S(2)}) copy-start(bf16[16,8,32,128]{3,2,1,0:T(8,128)(2,1)} %recycled.1) | copy-start | bytes 3145732
where the time goes:
time: 32.9 us; the launch traced here: 32.7 us
  starting transfers between devices  11.5 us (35%)
  blocking collectives  10.5 us (32%)
  Pallas kernels  7.25 us (22%)
  waiting for transfers between devices  2.74 us (8%)
  between operations  0.7 us (2%)
    all_to_all x1, blocking collectives, body(): parts = lax.all_to_all(parts, AXES, 0, 0)  10.5 us
    ppermute x5, starting transfers between devices, shifted(): return lax.ppermute(values, axes, pairs)  7.48 us
    pallas_call x6, Pallas kernels, call(): pl.pallas_call(kernel, out_shape=tuple(out_shape), in_specs=[in_smem if o...  7.25 us
    ppermute x1, starting transfers between devices, body(): lax.ppermute(second, 'gy', [(i, (i - 1 + 2 * (i % 2)) % count) for i in r...  2.47 us
    ppermute x5, waiting for transfers between devices, shifted(): return lax.ppermute(values, axes, pairs)  1.7 us
    ppermute x1, starting transfers between devices, body(): first = lax.ppermute(first, 'gy', [(i, i ^ 1) for i in range(count)])  1.6 us
    ppermute x1, waiting for transfers between devices, body(): lax.ppermute(second, 'gy', [(i, (i - 1 + 2 * (i % 2)) % count) for i in r...  1.03 us
  transfers between devices with their start and end apart: 7, of which 3 were waited for; matrix products, arithmetic and copies ran while one was open for 0% of the time, Pallas kernels for 10%

commit v1 on v0

--- a/solution.py
+++ b/solution.py
@@ -57,7 +57,7 @@
         at += width
 
 
-def rim_kernel(direction, residual, diagonal, coupling, rim_out, after_out, before_out, coupling_out):
+def rim_kernel(parity, direction, residual, diagonal, coupling, rim_out, outward_out, inward_out, coupling_out):
     planes, rows, _ = direction.shape
     slot = lanes_of(rows) // RIM
     after = jnp.zeros((rows, LANES), jnp.float32)
@@ -78,8 +78,9 @@
             if plane >= planes - S:
                 after = jnp.where(slot == S * field + plane - planes + S, here, after)
         rim_out[field] = rim
-    after_out[...] = after
-    before_out[...] = before
+    even = parity[0] < 2
+    outward_out[...] = jnp.where(even, before, after)
+    inward_out[...] = jnp.where(even, after, before)
     vector = lax.broadcasted_iota(jnp.int32, (RECYCLED, LANES), 0)
     spread = (lanes_of(RECYCLED) // TILE == vector).astype(jnp.float32)
     coupling_out[...] = jnp.dot(
@@ -119,13 +120,15 @@
 
 
 def edge_kernel(
-    parity, direction, residual, diagonal, low, high, rim_next, rim_before, rim_low_next, rim_low_before, rim_high_next, rim_high_before, first_out, second_out, rim_out
+    parity, direction, residual, diagonal, low, high, rim_next, rim_before, outward_next, outward_before, inward_next, inward_before, first_out, second_out, rim_out
 ):
     planes, rows, _ = direction.shape
     lane = lanes_of(rows)
     nearer = lane % RIM < S
-    low_rim = jnp.where(nearer, rim_low_next[...], rim_low_before[...])
-    high_rim = jnp.where(nearer, rim_high_next[...], rim_high_before[...])
+    outward = jnp.where(nearer, outward_next[...], outward_before[...])
+    inward = jnp.where(nearer, inward_next[...], inward_before[...])
+    low_rim = jnp.where(parity[0] < 2, outward, inward)
+    high_rim = jnp.where(parity[0] < 2, inward, outward)
     for field in range(3):
         rim = jnp.where(nearer, rim_next[field], rim_before[field])
         rim = jnp.where(lane < SIDE, turn(low_rim, -SIDE * field, 1), rim)
@@ -134,7 +137,7 @@
     fields = (direction, residual, diagonal)
     row = rows_of(TILE)
 
-    even = parity[0] == 0
+    even = parity[0] & 1 == 0
     for index, tile in enumerate(packing(planes)):
         lower = jnp.zeros((TILE, LANES), jnp.float32)
         upper = jnp.zeros((TILE, LANES), jnp.float32)
@@ -324,7 +327,7 @@
     fields = (direction, residual, diagonal)
     row = rows_of(TILE)
     near = row < S
-    even = parity[0] == 0
+    even = parity[0] & 1 == 0
     halo = {}
     for index, tile in enumerate(packing(planes)):
         above = jnp.where(even, first[index], second[index])
@@ -529,15 +532,25 @@
             direction_out[plane, part] = found[2] - correction
 
 
-def shifted(values, shifts):
-    axes = tuple(shifts)
-    counts = [lax.axis_size(axis) for axis in axes]
+def onward(step):
+    return lambda index, count: (index + step) % count
+
+
+def inward(index, count):
+    return index ^ 1
+
+
+def outward(index, count):
+    return (index - 1 + 2 * (index % 2)) % count
+
+
+def moved(values, moves):
+    axes = tuple(moves)
     pairs = [(0, 0)]
-    for axis, count in zip(axes, counts):
+    for axis in axes:
+        count = lax.axis_size(axis)
         pairs = [
-            (source * count + i, target * count + (i + shifts[axis]) % count)
-            for source, target in pairs
-            for i in range(count)
+            (source * count + i, target * count + moves[axis](i, count)) for source, target in pairs for i in range(count)
         ]
     return lax.ppermute(values, axes, pairs)
 
@@ -560,7 +573,7 @@
 
 def body(residual, direction, diagonal, recycled, recycled_images, coupling_inverse):
     planes, rows, columns = residual.shape
-    if columns != LANES or rows != 4 * TILE or RIM * (planes + 2 * S) != LANES or lax.axis_size("gy") % 2:
+    if columns != LANES or rows != 4 * TILE or RIM * (planes + 2 * S) != LANES or lax.axis_size("gx") % 2 or lax.axis_size("gy") % 2:
         raise ValueError("unsupported block")
     shape = residual.shape
     shifts, rim_shifts, groups = shift_matrices()
@@ -572,25 +585,25 @@
         [pltpu.SemaphoreType.DMA((4,))],
         in_hbm=(direction, residual, diagonal, coupling_inverse),
     )
-    low = shifted(upper, {"gx": 1})
-    high = shifted(lower, {"gx": -1})
-    rim, rim_after, rim_before, coupling = call(
-        rim_kernel, [(3, rows, LANES), (rows, LANES), (rows, LANES), (RECYCLED, LANES)], (*fields, coupling)
-    )
-    sides = (-1,) if lax.axis_size("gz") == 2 else (-1, 1)
-    rims = [shifted(rim, {"gz": side}) for side in sides]
-    low_rims = [shifted(rim_after, {"gx": 1, "gz": side}) for side in sides]
-    high_rims = [shifted(rim_before, {"gx": -1, "gz": side}) for side in sides]
-    parity = (lax.axis_index("gy") & 1).astype(jnp.int32).reshape(1)
+    parity = ((lax.axis_index("gy") & 1) + 2 * (lax.axis_index("gx") & 1)).astype(jnp.int32).reshape(1)
+    low = moved(upper, {"gx": onward(1)})
+    high = moved(lower, {"gx": onward(-1)})
+    rim, rim_outward, rim_inward, coupling = call(
+        rim_kernel, [(3, rows, LANES), (rows, LANES), (rows, LANES), (RECYCLED, LANES)], (parity, *fields, coupling)
+    )
+    sides = [onward(-1)] if lax.axis_size("gz") == 2 else [onward(-1), onward(1)]
+    outward_rims = [moved(rim_outward, {"gx": outward, "gz": side}) for side in sides]
+    rims = [moved(rim, {"gz": side}) for side in sides]
+    inward_rims = [moved(rim_inward, {"gx": inward, "gz": side}) for side in sides]
     tiles = len(packing(planes))
     first, second, whole_rims = call(
         edge_kernel,
         [(tiles, TILE, LANES), (tiles, TILE, LANES), (3, rows, LANES)],
-        (parity, *fields, low, high, rims[0], rims[-1], low_rims[0], low_rims[-1], high_rims[0], high_rims[-1]),
-    )
-    count = lax.axis_size("gy")
-    second = lax.ppermute(second, "gy", [(i, (i - 1 + 2 * (i % 2)) % count) for i in range(count)])
-    first = lax.ppermute(first, "gy", [(i, i ^ 1) for i in range(count)])
+        (parity, *fields, low, high, rims[0], rims[-1], outward_rims[0], outward_rims[-1])
+        + (inward_rims[0], inward_rims[-1]),
+    )
+    second = moved(second, {"gy": outward})
+    first = moved(first, {"gy": inward})
     devices = lax.axis_size(AXES)
     wide = planes + 2 * S
     worked = 2 * planes + 2 * (S - 1) + 2 * (S - 2)

time: 32.9 us -> 32.6 us (level)
  waiting for transfers between devices: 2.74 us -> 2.23 us
    ppermute x7, waiting for transfers between devices: 2.74 us -> 2.23 us  [moved(): return lax.ppermute(values, axes, pairs)]
where the time goes in v1:
time: 32.6 us; the launch traced here: 32.4 us
  starting transfers between devices  11.6 us (36%)
  blocking collectives  10.6 us (33%)
  Pallas kernels  7.25 us (22%)
  waiting for transfers between devices  2.23 us (7%)
  between operations  0.68 us (2%)
    ppermute x7, starting transfers between devices, moved(): return lax.ppermute(values, axes, pairs)  11.6 us
    all_to_all x1, blocking collectives, body(): parts = lax.all_to_all(parts, AXES, 0, 0)  10.6 us
    pallas_call x6, Pallas kernels, call(): pl.pallas_call(kernel, out_shape=tuple(out_shape), in_specs=[in_smem if o...  7.25 us
    ppermute x7, waiting for transfers between devices, moved(): return lax.ppermute(values, axes, pairs)  2.23 us
  transfers between devices with their start and end apart: 7, of which 3 were waited for; matrix products, arithmetic and copies ran while one was open for 0% of the time, Pallas kernels for 10%

profile of v1, /device:TPU:0, one launch (start us, length us, event | category | flops | bytes accessed | tf_op | source)
XLA Modules:
  0.0 32.4 jit_solution(2943774216868605999)
XLA Ops:
  0.6 1.1 %shard_map.112 = (f32[8,32,128]{2,1,0:T(8,128)S(1)}, f32[8,32,128]{2,1,0:T(8,128)S(1)}, f32[8,32,128]{2,1,0:T(8,128)S(1)}, f32[10,32,128]{2,1,0:T(8,128)S(1)}, f...) custom-call(f32[8,32,128]{2,1,0:T(8,128)} %direction_in.1, f32[8,32,128]{2,1,0:T(8,128)} %residual_in.1, ...), custom_call_target="tpu_custom_call" | custom-call | tf_op jit(solution)/shard_map/pallas_call | solution.py:564
  1.7 0.5 %collective-permute-start = (f32[10,32,128]{2,1,0:T(8,128)S(1)}, f32[10,32,128]{2,1,0:T(8,128)S(1)}, u32[]{:S(2)}, u32[]{:S(2)}) collective-permute-start(f32[10,32,128]{2,1,0:T(8,128)S(1)} %get-tuple-element.29), channel_id=1, source_target_pairs={{0,8},{8,16},{16,24},{24,0},{1,9},{9,17},{17,25},{25,1},{2,10},{10... | collective-permute-start | bytes 491528 | tf_op jit(solution)/shard_map/ppermute | solution.py:555
  2.3 2.0 %collective-permute-start.1 = (f32[10,32,128]{2,1,0:T(8,128)S(1)}, f32[10,32,128]{2,1,0:T(8,128)S(1)}, u32[]{:S(2)}, u32[]{:S(2)}) collective-permute-start(f32[10,32,128]{2,1,0:T(8,128)S(1)} %get-tuple-element.30), channel_id=1, source_target_pairs={{0,24},{8,0},{16,8},{24,16},{1,25},{9,1},{17,9},{25,17},{2,26},{10... | collective-permute-start | bytes 491528 | tf_op jit(solution)/shard_map/ppermute | solution.py:555
  4.3 0.3 shard_map.113
  4.5 2.3 %collective-permute-start.2 = (f32[3,32,128]{2,1,0:T(8,128)S(1)}, f32[3,32,128]{2,1,0:T(8,128)S(1)}, u32[]{:S(2)}, u32[]{:S(2)}) collective-permute-start(f32[3,32,128]{2,1,0:T(8,128)S(1)} %get-tuple-element.32), channel_id=1, source_target_pairs={{0,1},{1,0},{2,3},{3,2},{4,5},{5,4},{6,7},{7,6},{8,9},{9,8},{10,11... | collective-permute-start | bytes 147464 | tf_op jit(solution)/shard_map/ppermute | solution.py:555
  6.8 0.0 collective-permute-start.3
  6.8 0.0 copy-start.1
  6.8 0.0 copy-start.2
  6.8 2.7 %collective-permute-start.4 = (f32[32,128]{1,0:T(8,128)S(1)}, f32[32,128]{1,0:T(8,128)S(1)}, u32[]{:S(2)}, u32[]{:S(2)}) collective-permute-start(f32[32,128]{1,0:T(8,128)S(1)} %get-tuple-element.34), channel_id=1, source_target_pairs={{0,9},{1,8},{8,1},{9,0},{16,25},{17,24},{24,17},{25,16},{2,11},{3,... | collective-permute-start | bytes 49160 | tf_op jit(solution)/shard_map/ppermute | solution.py:555
  9.5 1.4 %collective-permute-done.3.outward_next.outward_before = f32[32,128]{1,0:T(8,128)S(1)} collective-permute-done((f32[32,128]{1,0:T(8,128)S(1)}, f32[32,128]{1,0:T(8,128)S(1)}, u32[]{:S(2)}, u32[]{:S(2)}) %collective-permute-start.3) | collective-permute-done | bytes 16416 | tf_op jit(solution)/shard_map/ppermute | solution.py:555
  10.9 0.2 collective-permute-done.4.inward_next.inward_before
  11.1 0.0 collective-permute-done.2.rim_next.rim_before
  11.1 0.0 collective-permute-done.low
  11.1 0.0 collective-permute-done.1.high
  11.1 0.1 shard_map.114
  11.2 1.6 %collective-permute-start.5 = (f32[14,8,128]{2,1,0:T(8,128)S(1)}, f32[14,8,128]{2,1,0:T(8,128)S(1)}, u32[]{:S(2)}, u32[]{:S(2)}) collective-permute-start(f32[14,8,128]{2,1,0:T(8,128)S(1)} %get-tuple-element.36), channel_id=1, source_target_pairs={{0,2},{2,0},{4,6},{6,4},{1,3},{3,1},{5,7},{7,5},{8,10},{10,8},{12,... | collective-permute-start | bytes 172040 | tf_op jit(solution)/shard_map/ppermute | solution.py:555
  12.9 2.5 %collective-permute-start.6 = (f32[14,8,128]{2,1,0:T(8,128)S(1)}, f32[14,8,128]{2,1,0:T(8,128)S(1)}, u32[]{:S(2)}, u32[]{:S(2)}) collective-permute-start(f32[14,8,128]{2,1,0:T(8,128)S(1)} %get-tuple-element.37), channel_id=1, source_target_pairs={{0,6},{2,4},{4,2},{6,0},{1,7},{3,5},{5,3},{7,1},{8,14},{10,12},{12... | collective-permute-start | bytes 172040 | tf_op jit(solution)/shard_map/ppermute | solution.py:555
  15.3 0.0 copy-done.1
  15.4 0.0 copy-done.2
  15.4 0.0 copy-start.3
  15.4 2.9 %shard_map.115 = (f32[7,8,32,128]{3,2,1,0:T(8,128)S(1)}, f32[24,8,128]{2,1,0:T(8,128)S(1)}, f32[144,256]{1,0:T(8,128)S(1)}, f32[4,16,32,128]{3,2,1,0:T(8,128)S(1...) custom-call(f32[8,32,128]{2,1,0:T(8,128)S(1)} %get-tuple-element.26., ...), custom_call_target="tpu_custom_call" | custom-call | tf_op jit(solution)/shard_map/pallas_call | solution.py:564
  18.3 0.0 collective-permute-done.5.first
  18.3 0.6 %collective-permute-done.6.second = f32[14,8,128]{2,1,0:T(8,128)S(1)} collective-permute-done((f32[14,8,128]{2,1,0:T(8,128)S(1)}, f32[14,8,128]{2,1,0:T(8,128)S(1)}, u32[]{:S(2)}, u32[]{:S(2)}) %collective-permute-start.6) | collective-permute-done | bytes 57376 | tf_op jit(solution)/shard_map/ppermute | solution.py:555
  18.9 0.0 copy-done.3
  19.0 0.0 copy-start
  19.0 1.4 %shard_map.116 = (f32[7,8,8,128]{3,2,1,0:T(8,128)S(1)}, f32[32,2,128]{2,1,0:T(2,128)S(1)}) custom-call(s32[1]{0:T(128)} %bitcast.parity, f32[8,32,128]{2,1,0:T(8,128)S(1)} %get-tuple-element.26.direction, f32[8,32,128]{2,1,0:T(8,128)S(1)} %get-tuple-element.27.residual, f32[8,32,128]{2,1,0:T(8,128)S(1)} %get-tuple-element.28.diagonal, ...), custom_call_target="tpu_custom_call" | custom-call | tf_op jit(solution)/shard_map/pallas_call | solution.py:564
  20.4 10.6 %all_to_all.5.parts = f32[32,2,128]{2,1,0:T(2,128)S(1)} all-to-all(f32[32,2,128]{2,1,0:T(2,128)S(1)} %get-tuple-element.45), channel_id=1, replica_groups=mesh['gx'=4,'gy'=4,'gz'=2] {'gx','gy','gz'}, dimensions={0} | all-to-all | bytes 65536 | tf_op jit(solution)/shard_map/all_to_all | solution.py:640
  30.9 0.0 copy-done
  30.9 1.4 %shard_map.117 = (f32[8,32,128]{2,1,0:T(8,128)}, f32[8,32,128]{2,1,0:T(8,128)}, f32[8,32,128]{2,1,0:T(8,128)}) custom-call(f32[32,2,128]{2,1,0:T(2,128)S(1)} %all_to_all.5.parts, f32[16,128]{1,0:T(8,128)S(1)} %get-tuple-element.46.coupling, f32[8,32,128]{2,1,0:T(8,128)S(1)} %get-tuple-element.26.direction, f32[8,32,128]{2,1,0:T(8,128)S(1)} %get-tuple-element.27.residual, ...), custom_call_target="tpu_custom_call" | custom-call | tf_op jit(solution)/shard_map/pallas_call | solution.py:564
Async XLA Ops:
  1.7 9.4 %collective-permute-start = (f32[10,32,128]{2,1,0:T(8,128)S(1)}, f32[10,32,128]{2,1,0:T(8,128)S(1)}, u32[]{:S(2)}, u32[]{:S(2)}) collective-permute-start(f32[10,32,128]{2,1,0:T(8,128)S(1)} %get-tuple-element.29), channel_id=1, source_target_pairs={{0,8},{8,16},{16,24},{24,0},{1,9},{9,17},{17,25},{25,1},{2,10},{10... | collective-permute-start | bytes 491528 | tf_op jit(solution)/shard_map/ppermute | solution.py:555
  2.3 8.9 %collective-permute-start.1 = (f32[10,32,128]{2,1,0:T(8,128)S(1)}, f32[10,32,128]{2,1,0:T(8,128)S(1)}, u32[]{:S(2)}, u32[]{:S(2)}) collective-permute-start(f32[10,32,128]{2,1,0:T(8,128)S(1)} %get-tuple-element.30), channel_id=1, source_target_pairs={{0,24},{8,0},{16,8},{24,16},{1,25},{9,1},{17,9},{25,17},{2,26},{10... | collective-permute-start | bytes 491528 | tf_op jit(solution)/shard_map/ppermute | solution.py:555
  4.5 6.6 %collective-permute-start.2 = (f32[3,32,128]{2,1,0:T(8,128)S(1)}, f32[3,32,128]{2,1,0:T(8,128)S(1)}, u32[]{:S(2)}, u32[]{:S(2)}) collective-permute-start(f32[3,32,128]{2,1,0:T(8,128)S(1)} %get-tuple-element.32), channel_id=1, source_target_pairs={{0,1},{1,0},{2,3},{3,2},{4,5},{5,4},{6,7},{7,6},{8,9},{9,8},{10,11... | collective-permute-start | bytes 147464 | tf_op jit(solution)/shard_map/ppermute | solution.py:555
  6.8 4.1 %collective-permute-start.3 = (f32[32,128]{1,0:T(8,128)S(1)}, f32[32,128]{1,0:T(8,128)S(1)}, u32[]{:S(2)}, u32[]{:S(2)}) collective-permute-start(f32[32,128]{1,0:T(8,128)S(1)} %get-tuple-element.33), channel_id=1, source_target_pairs={{0,25},{1,24},{8,17},{9,16},{16,9},{17,8},{24,1},{25,0},{2,27},{3,... | collective-permute-start | bytes 49160 | tf_op jit(solution)/shard_map/ppermute | solution.py:555
  6.8 8.5 %copy-start.1 = (bf16[512,256]{1,0:T(8,128)(2,1)S(1)}, bf16[512,256]{1,0:T(8,128)(2,1)}, u32[]{:S(2)}) copy-start(bf16[512,256]{1,0:T(8,128)(2,1)} %constant.19.clone.shifts) | copy-start | bytes 786436
  6.8 8.5 %copy-start.2 = (bf16[256,128]{1,0:T(8,128)(2,1)S(1)}, bf16[256,128]{1,0:T(8,128)(2,1)}, u32[]{:S(2)}) copy-start(bf16[256,128]{1,0:T(8,128)(2,1)} %constant.20.clone.rim_shifts) | copy-start | bytes 196612
  6.8 4.3 %collective-permute-start.4 = (f32[32,128]{1,0:T(8,128)S(1)}, f32[32,128]{1,0:T(8,128)S(1)}, u32[]{:S(2)}, u32[]{:S(2)}) collective-permute-start(f32[32,128]{1,0:T(8,128)S(1)} %get-tuple-element.34), channel_id=1, source_target_pairs={{0,9},{1,8},{8,1},{9,0},{16,25},{17,24},{24,17},{25,16},{2,11},{3,... | collective-permute-start | bytes 49160 | tf_op jit(solution)/shard_map/ppermute | solution.py:555
  11.2 7.1 %collective-permute-start.5 = (f32[14,8,128]{2,1,0:T(8,128)S(1)}, f32[14,8,128]{2,1,0:T(8,128)S(1)}, u32[]{:S(2)}, u32[]{:S(2)}) collective-permute-start(f32[14,8,128]{2,1,0:T(8,128)S(1)} %get-tuple-element.36), channel_id=1, source_target_pairs={{0,2},{2,0},{4,6},{6,4},{1,3},{3,1},{5,7},{7,5},{8,10},{10,8},{12,... | collective-permute-start | bytes 172040 | tf_op jit(solution)/shard_map/ppermute | solution.py:555
  12.9 6.1 %collective-permute-start.6 = (f32[14,8,128]{2,1,0:T(8,128)S(1)}, f32[14,8,128]{2,1,0:T(8,128)S(1)}, u32[]{:S(2)}, u32[]{:S(2)}) collective-permute-start(f32[14,8,128]{2,1,0:T(8,128)S(1)} %get-tuple-element.37), channel_id=1, source_target_pairs={{0,6},{2,4},{4,2},{6,0},{1,7},{3,5},{5,3},{7,1},{8,14},{10,12},{12... | collective-permute-start | bytes 172040 | tf_op jit(solution)/shard_map/ppermute | solution.py:555
  15.4 3.6 %copy-start.3 = (bf16[768,128]{1,0:T(8,128)(2,1)S(1)}, bf16[768,128]{1,0:T(8,128)(2,1)}, u32[]{:S(2)}) copy-start(bf16[768,128]{1,0:T(8,128)(2,1)} %constant.21.clone.groups) | copy-start | bytes 589828
  19.0 12.0 %copy-start = (bf16[16,8,32,128]{3,2,1,0:T(8,128)(2,1)S(1)}, bf16[16,8,32,128]{3,2,1,0:T(8,128)(2,1)}, u32[]{:S(2)}) copy-start(bf16[16,8,32,128]{3,2,1,0:T(8,128)(2,1)} %recycled.1) | copy-start | bytes 3145732

commit v2 on v1

--- a/solution.py
+++ b/solution.py
@@ -78,7 +78,7 @@
             if plane >= planes - S:
                 after = jnp.where(slot == S * field + plane - planes + S, here, after)
         rim_out[field] = rim
-    even = parity[0] < 2
+    even = parity[0] & 2 == 0
     outward_out[...] = jnp.where(even, before, after)
     inward_out[...] = jnp.where(even, after, before)
     vector = lax.broadcasted_iota(jnp.int32, (RECYCLED, LANES), 0)
@@ -127,8 +127,8 @@
     nearer = lane % RIM < S
     outward = jnp.where(nearer, outward_next[...], outward_before[...])
     inward = jnp.where(nearer, inward_next[...], inward_before[...])
-    low_rim = jnp.where(parity[0] < 2, outward, inward)
-    high_rim = jnp.where(parity[0] < 2, inward, outward)
+    low_rim = jnp.where(parity[0] & 2 == 0, outward, inward)
+    high_rim = jnp.where(parity[0] & 2 == 0, inward, outward)
     for field in range(3):
         rim = jnp.where(nearer, rim_next[field], rim_before[field])
         rim = jnp.where(lane < SIDE, turn(low_rim, -SIDE * field, 1), rim)
@@ -275,12 +275,11 @@
     return sums, total
 
 
-def inner_kernel(
-    direction, residual, diagonal, low, high, rims, shifts, rim_shifts, images_in, basis_out, sums_out, total_out, walk, trail, rim_walk, rim_trail, images, weight, left, done
+def steps_kernel(
+    direction, residual, diagonal, low, high, rims, shifts, rim_shifts, images_in, basis_out, walk, trail, rim_walk, rim_trail, images, weight, left, done
 ):
     planes, rows, _ = direction.shape
     fields = (direction, residual, diagonal)
-    row = rows_of(TILE)
     copy = pltpu.make_async_copy(images_in, images, done)
     copy.start()
 
@@ -297,19 +296,23 @@
         (rim_trail if field else rim_walk)[level] = values
 
     march(load, vertical, planes, rows, walk, trail, weight, left, shifts, rim_shifts, emit, keep)
+    copy.wait()
+
+
+def products_kernel(direction, residual, basis, images, sums_out, total_out):
+    planes, rows, _ = direction.shape
+    row = rows_of(TILE)
 
     def tiles_of(index, x):
         if index in (0, S + 1):
-            values = fields[index > 0][x]
+            values = (residual if index else direction)[x]
         else:
-            values = basis_out[index - 1 if index <= S else index - 2, x]
+            values = basis[index - 1 if index <= S else index - 2, x]
         tiles = [values[start : start + TILE] for start in range(0, rows, TILE)]
         tiles[0] = jnp.where(row < S, 0.0, tiles[0])
         tiles[-1] = jnp.where(row < S, tiles[-1], 0.0)
         return tiles
 
-    copy.wait()
-
     def images_of(x):
         return [images[:, x, start : start + 2 * TILE] for start in range(0, rows, 2 * TILE)]
 
@@ -320,7 +323,7 @@
 
 
 def caps_kernel(
-    parity, direction, residual, diagonal, low, high, rims, first, second, images, shifts, rim_shifts, groups, sums_in, total_in, inner_walk, inner_trail, inner_rim_walk, inner_rim_trail, caps_out, parts_out, walk, trail, weight, left
+    parity, direction, residual, diagonal, low, high, rims, first, second, wrapped, images, shifts, rim_shifts, groups, sums_in, total_in, inner_walk, inner_trail, inner_rim_walk, inner_rim_trail, caps_out, parts_out, walk, trail, weight, left
 ):
     planes, rows, _ = direction.shape
     ring = 2 * TILE
@@ -329,9 +332,11 @@
     near = row < S
     even = parity[0] & 1 == 0
     halo = {}
+    at_end = parity[0] >= 4
     for index, tile in enumerate(packing(planes)):
-        above = jnp.where(even, first[index], second[index])
-        below = jnp.where(even, second[index], first[index])
+        other = jnp.where(at_end, wrapped[index], second[index])
+        above = jnp.where(even, first[index], other)
+        below = jnp.where(even, other, first[index])
         for count, field, x, offset in tile:
             halo[field, x] = jnp.where(near, turn(above, -offset, 0), turn(below, -offset - count, 0))
     nothing = jnp.zeros((TILE, LANES), jnp.float32)
@@ -573,7 +578,7 @@
 
 def body(residual, direction, diagonal, recycled, recycled_images, coupling_inverse):
     planes, rows, columns = residual.shape
-    if columns != LANES or rows != 4 * TILE or RIM * (planes + 2 * S) != LANES or lax.axis_size("gx") % 2 or lax.axis_size("gy") % 2:
+    if columns != LANES or rows != 4 * TILE or RIM * (planes + 2 * S) != LANES or lax.axis_size("gx") % 2 or lax.axis_size("gy") % 4:
         raise ValueError("unsupported block")
     shape = residual.shape
     shifts, rim_shifts, groups = shift_matrices()
@@ -585,7 +590,10 @@
         [pltpu.SemaphoreType.DMA((4,))],
         in_hbm=(direction, residual, diagonal, coupling_inverse),
     )
-    parity = ((lax.axis_index("gy") & 1) + 2 * (lax.axis_index("gx") & 1)).astype(jnp.int32).reshape(1)
+    count = lax.axis_size("gy")
+    y = lax.axis_index("gy")
+    at_end = 4 * ((y == 0) | (y == count - 1)).astype(jnp.int32)
+    parity = ((y & 1) + 2 * (lax.axis_index("gx") & 1) + at_end).astype(jnp.int32).reshape(1)
     low = moved(upper, {"gx": onward(1)})
     high = moved(lower, {"gx": onward(-1)})
     rim, rim_outward, rim_inward, coupling = call(
@@ -602,23 +610,17 @@
         (parity, *fields, low, high, rims[0], rims[-1], outward_rims[0], outward_rims[-1])
         + (inward_rims[0], inward_rims[-1]),
     )
-    second = moved(second, {"gy": outward})
-    first = moved(first, {"gy": inward})
-    devices = lax.axis_size(AXES)
     wide = planes + 2 * S
     worked = 2 * planes + 2 * (S - 1) + 2 * (S - 2)
 
     def weights_and_left(ring):
         return [pltpu.VMEM((wide, ring, LANES), jnp.float32), pltpu.VMEM((worked * ring, 4 * LANES), jnp.bfloat16)]
 
-    count = sum(len(family) for family in products())
-    block = 2 * TILE
-    basis, sums, total, *levels, images = call(
-        inner_kernel,
+    wrapped = lax.ppermute(second, "gy", [(0, count - 1), (count - 1, 0)])
+    basis, *levels, images = call(
+        steps_kernel,
         [
             (BASIS - 2, *shape),
-            (count, TILE, LANES),
-            (BASIS * block, RECYCLED * block),
             (S, wide, rows, LANES),
             (S - 1, wide, rows, LANES),
             (S, rows, LANES),
@@ -629,10 +631,18 @@
         weights_and_left(rows) + [pltpu.SemaphoreType.DMA],
         in_hbm=(recycled_images,),
     )
+    first = moved(first, {"gy": inward})
+    second = lax.ppermute(second, "gy", [(i, outward(i, count)) for i in range(1, count - 1)])
+    block = 2 * TILE
+    sums, total = call(
+        products_kernel,
+        [(sum(len(family) for family in products()), TILE, LANES), (BASIS * block, RECYCLED * block)],
+        (*fields[:2], basis, images),
+    )
     caps, parts = call(
         caps_kernel,
-        [(BASIS - 2, planes, TILE, LANES), (devices, 2, LANES)],
-        (parity, *fields, low, high, whole_rims, first, second, images)
+        [(BASIS - 2, planes, TILE, LANES), (lax.axis_size(AXES), 2, LANES)],
+        (parity, *fields, low, high, whole_rims, first, second, wrapped, images)
         + (shifts, rim_shifts, groups, sums, total, *levels),
         [pltpu.VMEM((S, wide, block, LANES), jnp.float32), pltpu.VMEM((S - 1, wide, block, LANES), jnp.float32)]
         + weights_and_left(block),

time: 32.6 us -> 34.6 us (1.061)
  starting transfers between devices: 11.6 us -> 14.2 us
  Pallas kernels: 7.25 us -> 6.46 us
    ppermute x0 -> x2, starting transfers between devices: none -> 5.03 us  [the longest x1 4.37 us: body(): wrapped = lax.ppermute(second, 'gy', [(0, count - 1), (count - 1, 0)])]
    ppermute x7 -> x6, starting transfers between devices: 11.6 us -> 9.17 us  [moved(): return lax.ppermute(values, axes, pairs)]
    pallas_call x6 -> x7, Pallas kernels: 7.25 us -> 6.46 us  [call(): pl.pallas_call(kernel, out_shape=tuple(out_shape), in_specs=[in_smem if o...]
    ppermute x0 -> x2, waiting for transfers between devices: none -> 0.65 us  [the longest x1 0.65 us: body(): wrapped = lax.ppermute(second, 'gy', [(0, count - 1), (count - 1, 0)])]
    ppermute x7 -> x6, waiting for transfers between devices: 2.23 us -> 1.6 us  [moved(): return lax.ppermute(values, axes, pairs)]
  transfers between devices with their start and end apart: 7 -> 8, of which waited for: 3 -> 3; matrix products, arithmetic and copies ran while one was open for 0% -> 0% of each run, Pallas kernels for 10% -> 7%
where the time goes in v2:
time: 34.6 us; the launch traced here: 34.4 us
  starting transfers between devices  14.2 us (41%)
  blocking collectives  10.7 us (31%)
  Pallas kernels  6.46 us (19%)
  waiting for transfers between devices  2.25 us (7%)
  between operations  0.73 us (2%)
    all_to_all x1, blocking collectives, body(): parts = lax.all_to_all(parts, AXES, 0, 0)  10.7 us
    ppermute x6, starting transfers between devices, moved(): return lax.ppermute(values, axes, pairs)  9.17 us
    pallas_call x7, Pallas kernels, call(): pl.pallas_call(kernel, out_shape=tuple(out_shape), in_specs=[in_smem if o...  6.46 us
    ppermute x1, starting transfers between devices, body(): wrapped = lax.ppermute(second, 'gy', [(0, count - 1), (count - 1, 0)])  4.37 us
    ppermute x6, waiting for transfers between devices, moved(): return lax.ppermute(values, axes, pairs)  1.6 us
  transfers between devices with their start and end apart: 8, of which 3 were waited for; matrix products, arithmetic and copies ran while one was open for 0% of the time, Pallas kernels for 7%

profile of v2, /device:TPU:0, one launch (start us, length us, event | category | flops | bytes accessed | tf_op | source)
XLA Modules:
  0.0 34.4 jit_solution(8180708434902956088)
XLA Ops:
  0.6 1.1 %shard_map.112 = (f32[8,32,128]{2,1,0:T(8,128)S(1)}, f32[8,32,128]{2,1,0:T(8,128)S(1)}, f32[8,32,128]{2,1,0:T(8,128)S(1)}, f32[10,32,128]{2,1,0:T(8,128)S(1)}, f...) custom-call(f32[8,32,128]{2,1,0:T(8,128)} %direction_in.1, f32[8,32,128]{2,1,0:T(8,128)} %residual_in.1, ...), custom_call_target="tpu_custom_call" | custom-call | tf_op jit(solution)/shard_map/pallas_call | solution.py:569
  1.7 0.5 %collective-permute-start = (f32[10,32,128]{2,1,0:T(8,128)S(1)}, f32[10,32,128]{2,1,0:T(8,128)S(1)}, u32[]{:S(2)}, u32[]{:S(2)}) collective-permute-start(f32[10,32,128]{2,1,0:T(8,128)S(1)} %get-tuple-element.29), channel_id=1, source_target_pairs={{0,8},{8,16},{16,24},{24,0},{1,9},{9,17},{17,25},{25,1},{2,10},{10... | collective-permute-start | bytes 491528 | tf_op jit(solution)/shard_map/ppermute | solution.py:560
  2.3 2.0 %collective-permute-start.1 = (f32[10,32,128]{2,1,0:T(8,128)S(1)}, f32[10,32,128]{2,1,0:T(8,128)S(1)}, u32[]{:S(2)}, u32[]{:S(2)}) collective-permute-start(f32[10,32,128]{2,1,0:T(8,128)S(1)} %get-tuple-element.30), channel_id=1, source_target_pairs={{0,24},{8,0},{16,8},{24,16},{1,25},{9,1},{17,9},{25,17},{2,26},{10... | collective-permute-start | bytes 491528 | tf_op jit(solution)/shard_map/ppermute | solution.py:560
  4.3 0.3 shard_map.113
  4.5 2.3 %collective-permute-start.2 = (f32[3,32,128]{2,1,0:T(8,128)S(1)}, f32[3,32,128]{2,1,0:T(8,128)S(1)}, u32[]{:S(2)}, u32[]{:S(2)}) collective-permute-start(f32[3,32,128]{2,1,0:T(8,128)S(1)} %get-tuple-element.32), channel_id=1, source_target_pairs={{0,1},{1,0},{2,3},{3,2},{4,5},{5,4},{6,7},{7,6},{8,9},{9,8},{10,11... | collective-permute-start | bytes 147464 | tf_op jit(solution)/shard_map/ppermute | solution.py:560
  6.8 0.0 collective-permute-start.3
  6.8 0.0 copy-start.1
  6.8 0.0 copy-start.2
  6.8 2.7 %collective-permute-start.4 = (f32[32,128]{1,0:T(8,128)S(1)}, f32[32,128]{1,0:T(8,128)S(1)}, u32[]{:S(2)}, u32[]{:S(2)}) collective-permute-start(f32[32,128]{1,0:T(8,128)S(1)} %get-tuple-element.34), channel_id=1, source_target_pairs={{0,9},{1,8},{8,1},{9,0},{16,25},{17,24},{24,17},{25,16},{2,11},{3,... | collective-permute-start | bytes 49160 | tf_op jit(solution)/shard_map/ppermute | solution.py:560
  9.5 1.4 %collective-permute-done.3.outward_next.outward_before = f32[32,128]{1,0:T(8,128)S(1)} collective-permute-done((f32[32,128]{1,0:T(8,128)S(1)}, f32[32,128]{1,0:T(8,128)S(1)}, u32[]{:S(2)}, u32[]{:S(2)}) %collective-permute-start.3) | collective-permute-done | bytes 16416 | tf_op jit(solution)/shard_map/ppermute | solution.py:560
  10.9 0.2 collective-permute-done.4.inward_next.inward_before
  11.1 0.0 collective-permute-done.2.rim_next.rim_before
  11.1 0.0 collective-permute-done.low
  11.1 0.0 collective-permute-done.1.high
  11.1 0.1 shard_map.114
  11.2 1.6 %collective-permute-start.5 = (f32[14,8,128]{2,1,0:T(8,128)S(1)}, f32[14,8,128]{2,1,0:T(8,128)S(1)}, u32[]{:S(2)}, u32[]{:S(2)}) collective-permute-start(f32[14,8,128]{2,1,0:T(8,128)S(1)} %get-tuple-element.36), channel_id=1, source_target_pairs={{0,2},{2,0},{4,6},{6,4},{1,3},{3,1},{5,7},{7,5},{8,10},{10,8},{12,... | collective-permute-start | bytes 172040 | tf_op jit(solution)/shard_map/ppermute | solution.py:560
  12.9 4.4 %collective-permute-start.7 = (f32[14,8,128]{2,1,0:T(8,128)S(1)}, f32[14,8,128]{2,1,0:T(8,128)S(1)}, u32[]{:S(2)}, u32[]{:S(2)}) collective-permute-start(f32[14,8,128]{2,1,0:T(8,128)S(1)} %get-tuple-element.37), channel_id=1, source_target_pairs={{0,6},{6,0},{1,7},{7,1},{8,14},{14,8},{9,15},{15,9},{16,22},{22,16... | collective-permute-start | bytes 172040 | tf_op jit(solution)/shard_map/ppermute | solution.py:619
  17.3 0.7 %collective-permute-start.6 = (f32[14,8,128]{2,1,0:T(8,128)S(1)}, f32[14,8,128]{2,1,0:T(8,128)S(1)}, u32[]{:S(2)}, u32[]{:S(2)}) collective-permute-start(f32[14,8,128]{2,1,0:T(8,128)S(1)} %get-tuple-element.37), channel_id=1, source_target_pairs={{2,4},{4,2},{3,5},{5,3},{10,12},{12,10},{11,13},{13,11},{18,20},{2... | collective-permute-start | bytes 172040 | tf_op jit(solution)/shard_map/ppermute | solution.py:635
  17.9 0.0 copy-done.1
  17.9 0.0 copy-done.2
  17.9 1.5 %shard_map.115 = (f32[7,8,32,128]{3,2,1,0:T(8,128)S(1)}, f32[4,16,32,128]{3,2,1,0:T(8,128)S(1)}, f32[3,16,32,128]{3,2,1,0:T(8,128)S(1)}, f32[4,32,128]{2,1,0:T(8...) custom-call(f32[8,32,128]{2,1,0:T(8,128)S(1)} %get-tuple-element.26.direction, ...), custom_call_target="tpu_custom_call" | custom-call | tf_op jit(solution)/shard_map/pallas_call | solution.py:569
  19.5 0.0 copy-start.3
  19.5 0.6 %shard_map.116 = (f32[24,8,128]{2,1,0:T(8,128)S(1)}, f32[144,256]{1,0:T(8,128)S(1)}) custom-call(f32[8,32,128]{2,1,0:T(8,128)S(1)} %get-tuple-element.26.direction, f32[8,32,128]{2,1,0:T(8,128)S(1)} %get-tuple-element.27.residual, f32[7,8,32,128]{3,2,1,0:T(8,128)S(1)} %get-tuple-element.39.basis, bf16[16,8,32,128]{3,2,1,0:T(8,128)(2,1)S(1)} %get-tuple-element.38.images), custom_call_target="tpu_custom_call" | custom-call | tf_op jit(solution)/shard_map/pallas_call | solution.py:569
  20.1 0.0 collective-permute-done.5.first
  20.1 0.7 %collective-permute-done.7.wrapped = f32[14,8,128]{2,1,0:T(8,128)S(1)} collective-permute-done((f32[14,8,128]{2,1,0:T(8,128)S(1)}, f32[14,8,128]{2,1,0:T(8,128)S(1)}, u32[]{:S(2)}, u32[]{:S(2)}) %collective-permute-start.7) | collective-permute-done | bytes 57376 | tf_op jit(solution)/shard_map/ppermute | solution.py:619
  20.7 0.0 collective-permute-done.6.second
  20.7 0.0 copy-done.3
  20.7 0.0 copy-start
  20.8 1.5 %shard_map.117 = (f32[7,8,8,128]{3,2,1,0:T(8,128)S(1)}, f32[32,2,128]{2,1,0:T(2,128)S(1)}) custom-call(s32[1]{0:T(128)} %bitcast.parity, f32[8,32,128]{2,1,0:T(8,128)S(1)} %get-tuple-element.26.direction, f32[8,32,128]{2,1,0:T(8,128)S(1)} %get-tuple-element.27.residual, f32[8,32,128]{2,1,0:T(8,128)S(1)} %get-tuple-element.28.diagonal, ...), custom_call_target="tpu_custom_call" | custom-call | tf_op jit(solution)/shard_map/pallas_call | solution.py:569
  22.2 10.7 %all_to_all.5.parts = f32[32,2,128]{2,1,0:T(2,128)S(1)} all-to-all(f32[32,2,128]{2,1,0:T(2,128)S(1)} %get-tuple-element.46), channel_id=1, replica_groups=mesh['gx'=4,'gy'=4,'gz'=2] {'gx','gy','gz'}, dimensions={0} | all-to-all | bytes 65536 | tf_op jit(solution)/shard_map/all_to_all | solution.py:650
  33.0 0.0 copy-done
  33.0 1.4 %shard_map.118 = (f32[8,32,128]{2,1,0:T(8,128)}, f32[8,32,128]{2,1,0:T(8,128)}, f32[8,32,128]{2,1,0:T(8,128)}) custom-call(f32[32,2,128]{2,1,0:T(2,128)S(1)} %all_to_all.5.parts, f32[16,128]{1,0:T(8,128)S(1)} %get-tuple-element.47.coupling, f32[8,32,128]{2,1,0:T(8,128)S(1)} %get-tuple-element.26.direction, f32[8,32,128]{2,1,0:T(8,128)S(1)} %get-tuple-element.27.residual, ...), custom_call_target="tpu_custom_call" | custom-call | tf_op jit(solution)/shard_map/pallas_call | solution.py:569
Async XLA Ops:
  1.7 9.4 %collective-permute-start = (f32[10,32,128]{2,1,0:T(8,128)S(1)}, f32[10,32,128]{2,1,0:T(8,128)S(1)}, u32[]{:S(2)}, u32[]{:S(2)}) collective-permute-start(f32[10,32,128]{2,1,0:T(8,128)S(1)} %get-tuple-element.29), channel_id=1, source_target_pairs={{0,8},{8,16},{16,24},{24,0},{1,9},{9,17},{17,25},{25,1},{2,10},{10... | collective-permute-start | bytes 491528 | tf_op jit(solution)/shard_map/ppermute | solution.py:560
  2.3 8.9 %collective-permute-start.1 = (f32[10,32,128]{2,1,0:T(8,128)S(1)}, f32[10,32,128]{2,1,0:T(8,128)S(1)}, u32[]{:S(2)}, u32[]{:S(2)}) collective-permute-start(f32[10,32,128]{2,1,0:T(8,128)S(1)} %get-tuple-element.30), channel_id=1, source_target_pairs={{0,24},{8,0},{16,8},{24,16},{1,25},{9,1},{17,9},{25,17},{2,26},{10... | collective-permute-start | bytes 491528 | tf_op jit(solution)/shard_map/ppermute | solution.py:560
  4.5 6.6 %collective-permute-start.2 = (f32[3,32,128]{2,1,0:T(8,128)S(1)}, f32[3,32,128]{2,1,0:T(8,128)S(1)}, u32[]{:S(2)}, u32[]{:S(2)}) collective-permute-start(f32[3,32,128]{2,1,0:T(8,128)S(1)} %get-tuple-element.32), channel_id=1, source_target_pairs={{0,1},{1,0},{2,3},{3,2},{4,5},{5,4},{6,7},{7,6},{8,9},{9,8},{10,11... | collective-permute-start | bytes 147464 | tf_op jit(solution)/shard_map/ppermute | solution.py:560
  6.8 4.1 %collective-permute-start.3 = (f32[32,128]{1,0:T(8,128)S(1)}, f32[32,128]{1,0:T(8,128)S(1)}, u32[]{:S(2)}, u32[]{:S(2)}) collective-permute-start(f32[32,128]{1,0:T(8,128)S(1)} %get-tuple-element.33), channel_id=1, source_target_pairs={{0,25},{1,24},{8,17},{9,16},{16,9},{17,8},{24,1},{25,0},{2,27},{3,... | collective-permute-start | bytes 49160 | tf_op jit(solution)/shard_map/ppermute | solution.py:560
  6.8 11.1 %copy-start.1 = (bf16[512,256]{1,0:T(8,128)(2,1)S(1)}, bf16[512,256]{1,0:T(8,128)(2,1)}, u32[]{:S(2)}) copy-start(bf16[512,256]{1,0:T(8,128)(2,1)} %constant.26.clone.shifts) | copy-start | bytes 786436
  6.8 11.1 %copy-start.2 = (bf16[256,128]{1,0:T(8,128)(2,1)S(1)}, bf16[256,128]{1,0:T(8,128)(2,1)}, u32[]{:S(2)}) copy-start(bf16[256,128]{1,0:T(8,128)(2,1)} %constant.27.clone.rim_shifts) | copy-start | bytes 196612
  6.8 4.3 %collective-permute-start.4 = (f32[32,128]{1,0:T(8,128)S(1)}, f32[32,128]{1,0:T(8,128)S(1)}, u32[]{:S(2)}, u32[]{:S(2)}) collective-permute-start(f32[32,128]{1,0:T(8,128)S(1)} %get-tuple-element.34), channel_id=1, source_target_pairs={{0,9},{1,8},{8,1},{9,0},{16,25},{17,24},{24,17},{25,16},{2,11},{3,... | collective-permute-start | bytes 49160 | tf_op jit(solution)/shard_map/ppermute | solution.py:560
  11.2 8.8 %collective-permute-start.5 = (f32[14,8,128]{2,1,0:T(8,128)S(1)}, f32[14,8,128]{2,1,0:T(8,128)S(1)}, u32[]{:S(2)}, u32[]{:S(2)}) collective-permute-start(f32[14,8,128]{2,1,0:T(8,128)S(1)} %get-tuple-element.36), channel_id=1, source_target_pairs={{0,2},{2,0},{4,6},{6,4},{1,3},{3,1},{5,7},{7,5},{8,10},{10,8},{12,... | collective-permute-start | bytes 172040 | tf_op jit(solution)/shard_map/ppermute | solution.py:560
  12.9 7.9 %collective-permute-start.7 = (f32[14,8,128]{2,1,0:T(8,128)S(1)}, f32[14,8,128]{2,1,0:T(8,128)S(1)}, u32[]{:S(2)}, u32[]{:S(2)}) collective-permute-start(f32[14,8,128]{2,1,0:T(8,128)S(1)} %get-tuple-element.37), channel_id=1, source_target_pairs={{0,6},{6,0},{1,7},{7,1},{8,14},{14,8},{9,15},{15,9},{16,22},{22,16... | collective-permute-start | bytes 172040 | tf_op jit(solution)/shard_map/ppermute | solution.py:619
  17.3 3.5 %collective-permute-start.6 = (f32[14,8,128]{2,1,0:T(8,128)S(1)}, f32[14,8,128]{2,1,0:T(8,128)S(1)}, u32[]{:S(2)}, u32[]{:S(2)}) collective-permute-start(f32[14,8,128]{2,1,0:T(8,128)S(1)} %get-tuple-element.37), channel_id=1, source_target_pairs={{2,4},{4,2},{3,5},{5,3},{10,12},{12,10},{11,13},{13,11},{18,20},{2... | collective-permute-start | bytes 172040 | tf_op jit(solution)/shard_map/ppermute | solution.py:635
  19.5 1.2 %copy-start.3 = (bf16[768,128]{1,0:T(8,128)(2,1)S(1)}, bf16[768,128]{1,0:T(8,128)(2,1)}, u32[]{:S(2)}) copy-start(bf16[768,128]{1,0:T(8,128)(2,1)} %constant.28.clone.groups) | copy-start | bytes 589828
  20.7 12.2 %copy-start = (bf16[16,8,32,128]{3,2,1,0:T(8,128)(2,1)S(1)}, bf16[16,8,32,128]{3,2,1,0:T(8,128)(2,1)}, u32[]{:S(2)}) copy-start(bf16[16,8,32,128]{3,2,1,0:T(8,128)(2,1)} %recycled.1) | copy-start | bytes 3145732

commit v3 on v1

--- a/solution.py
+++ b/solution.py
@@ -88,15 +88,15 @@
     )
 
 
-def plane_of(own, low, high, field, x):
+def plane_of(own, low, high, field, x, part=slice(None)):
     planes = own.shape[0]
     first = (0, S, 2 * S - 1)[field]
     width = (S, S - 1, S - 1)[field]
     if x < 0:
-        return low[first + width + x]
+        return low[first + width + x, part]
     if x >= planes:
-        return high[first + x - planes]
-    return own[x]
+        return high[first + x - planes, part]
+    return own[x, part]
 
 
 def packing(planes):
@@ -209,12 +209,15 @@
             if reach < 0:
                 continue
             facing = [part.astype(jnp.float32) for part in split(rim_levels[field][level])]
-            for x in range(-reach, planes + reach):
-                parts = list(split(history[level, x + S]))
-                parts += [jnp.where(slot == x + S, part, 0.0).astype(jnp.bfloat16) for part in facing]
+            for x in range(-reach, planes + reach, 2):
+                both = (x, x + 1)
+                parts = split(jnp.concatenate([history[level, one + S] for one in both], axis=0))
+                for part in facing:
+                    slots = [jnp.where(slot == one + S, part, 0.0) for one in both]
+                    parts.append(jnp.concatenate(slots, axis=0).astype(jnp.bfloat16))
                 for index, part in enumerate(parts):
-                    left[ring * len(work) : ring * (len(work) + 1), LANES * index : LANES * (index + 1)] = part
-                work.append((field, history, offset, reach, x))
+                    left[ring * len(work) : ring * (len(work) + 2), LANES * index : LANES * (index + 1)] = part
+                work += [(field, history, offset, reach, one) for one in both]
         moved = jnp.dot(left[: ring * len(work)], shifts[...], preferred_element_type=jnp.float32)
         gathered = {}
         for index, (field, history, offset, reach, x) in enumerate(work):
@@ -319,45 +322,70 @@
     total_out[...] = total
 
 
+def cap_steps(
+    high_side, arrived, fields, low, high, rims, shifts, rim_shifts, inner_walk, inner_trail, inner_rim_walk, inner_rim_trail, walk, trail, weight, left, emit
+):
+    planes, rows, _ = fields[0].shape
+    row = rows_of(TILE)
+    near = row < S
+    side = jnp.where(high_side, 1, 0)
+    beyond_here = near == (jnp.zeros((TILE, LANES), jnp.int32) + side == 1)
+    from_above = (row == S) & (jnp.zeros((TILE, LANES), jnp.int32) + side == 0)
+    from_below = (row == S - 1) & (jnp.zeros((TILE, LANES), jnp.int32) + side == 1)
+    start = pl.multiple_of(side * (rows - TILE), TILE)
+    part = pl.ds(start, TILE)
+    halo = {}
+    for tile, pieces in enumerate(packing(planes)):
+        for count, field, x, offset in pieces:
+            message = arrived(tile)
+            halo[field, x] = jnp.where(high_side, turn(message, -offset, 0), turn(message, -offset - count, 0))
+    nothing = jnp.zeros((TILE, LANES), jnp.float32)
+
+    def load(field, x):
+        if x is None:
+            values = rims[field, part]
+        else:
+            values = plane_of(fields[field], low, high, field, x, part)
+        return jnp.where(beyond_here, halo.get((field, x), nothing), values)
+
+    def vertical(values, field, level, x):
+        if x is None:
+            known = (inner_rim_trail if field else inner_rim_walk)[level, part]
+        else:
+            known = (inner_trail if field else inner_walk)[level, x + S, part]
+        after = turn(jnp.where(from_above, known, values), -1, 0)
+        return after + turn(jnp.where(from_below, known, values), 1, 0)
+
+    march(load, vertical, planes, TILE, walk, trail, weight, left, shifts, rim_shifts, emit, lambda *_: None)
+
+
+def first_cap_kernel(
+    parity, direction, residual, diagonal, low, high, rims, first, shifts, rim_shifts, inner_walk, inner_trail, inner_rim_walk, inner_rim_trail, cap_out, walk, trail, weight, left
+):
+    def emit(index, x, values):
+        cap_out[index, x] = values
+
+    cap_steps(
+        parity[0] & 1 == 0, lambda tile: first[tile], (direction, residual, diagonal), low, high, rims, shifts, rim_shifts, inner_walk, inner_trail, inner_rim_walk, inner_rim_trail, walk, trail, weight, left, emit
+    )
+
+
 def caps_kernel(
-    parity, direction, residual, diagonal, low, high, rims, first, second, images, shifts, rim_shifts, groups, sums_in, total_in, inner_walk, inner_trail, inner_rim_walk, inner_rim_trail, caps_out, parts_out, walk, trail, weight, left
+    parity, direction, residual, diagonal, low, high, rims, second, cap, images, shifts, rim_shifts, groups, sums_in, total_in, inner_walk, inner_trail, inner_rim_walk, inner_rim_trail, caps_out, parts_out, walk, trail, weight, left
 ):
     planes, rows, _ = direction.shape
-    ring = 2 * TILE
     fields = (direction, residual, diagonal)
     row = rows_of(TILE)
     near = row < S
-    even = parity[0] & 1 == 0
-    halo = {}
-    for index, tile in enumerate(packing(planes)):
-        above = jnp.where(even, first[index], second[index])
-        below = jnp.where(even, second[index], first[index])
-        for count, field, x, offset in tile:
-            halo[field, x] = jnp.where(near, turn(above, -offset, 0), turn(below, -offset - count, 0))
-    nothing = jnp.zeros((TILE, LANES), jnp.float32)
-
-    def load(field, x):
-        values = rims[field] if x is None else plane_of(fields[field], low, high, field, x)
-        beyond = halo.get((field, x), nothing)
-        return jnp.concatenate(
-            [jnp.where(near, beyond, values[rows - TILE :]), jnp.where(near, values[:TILE], beyond)], axis=0
-        )
-
-    def vertical(values, field, level, x):
-        if x is None:
-            known = (inner_rim_trail if field else inner_rim_walk)[level]
-        else:
-            known = (inner_trail if field else inner_walk)[level, x + S]
-        top = values[:TILE]
-        bottom = values[TILE:]
-        top_sum = turn(top, -1, 0) + turn(jnp.where(row == S - 1, known[rows - TILE :], top), 1, 0)
-        bottom_sum = turn(jnp.where(row == S, known[:TILE], bottom), -1, 0) + turn(bottom, 1, 0)
-        return jnp.concatenate([top_sum, bottom_sum], axis=0)
+    odd = parity[0] & 1
+    ours = near == (jnp.zeros((TILE, LANES), jnp.int32) + odd == 0)
 
     def emit(index, x, values):
-        caps_out[index, x] = jnp.where(near, values[TILE:], values[:TILE])
-
-    march(load, vertical, planes, ring, walk, trail, weight, left, shifts, rim_shifts, emit, lambda *_: None)
+        caps_out[index, x] = jnp.where(ours, values, cap[index, x])
+
+    cap_steps(
+        odd == 1, lambda tile: second[tile], fields, low, high, rims, shifts, rim_shifts, inner_walk, inner_trail, inner_rim_walk, inner_rim_trail, walk, trail, weight, left, emit
+    )
 
     def tile_of(index, x):
         if index in (0, S + 1):
@@ -414,8 +442,9 @@
     table = jnp.concatenate(
         [jnp.sum(mixed, axis=0, keepdims=True), jnp.sum(extra, axis=0, keepdims=True)], axis=0
     )
-    for device in range(parts_out.shape[0]):
-        parts_out[device] = table
+    table = jnp.concatenate([table] * (TILE // 2), axis=0)
+    for start in range(0, parts_out.shape[0], TILE):
+        parts_out[start : start + TILE] = table
 
 
 def moments_of(values):
@@ -426,11 +455,16 @@
 def finish_kernel(
     parts, coupling, direction, residual, basis, caps, recycled, delta_out, residual_out, direction_out
 ):
-    table = jnp.sum(parts[...], axis=0)
+    pieces = [parts[start : start + TILE] for start in range(0, parts.shape[0], TILE)]
+    while len(pieces) > 1:
+        pieces = [a + b for a, b in zip(pieces[::2], pieces[1::2])] + pieces[len(pieces) // 2 * 2 :]
+    table = pieces[0]
+    for shift in (4, 2):
+        table = table + turn(table, shift, 0)
     spot = lanes_of(TILE)
     row = rows_of(TILE)
     mixed = jnp.broadcast_to(table[:1], (TILE, LANES))
-    extra = jnp.broadcast_to(table[1:], (TILE, LANES))
+    extra = jnp.broadcast_to(table[1:2], (TILE, LANES))
     columns = []
     for place in range(3):
         mine = (spot // TILE == row) & (spot % TILE == place + 1)
@@ -500,7 +534,12 @@
     projected = mixed * across + jnp.where(spot % TILE == 0, extra * residue[BASIS - 1], 0.0)
     projected = projected[:1]
     weights = jnp.sum(coupling[...] * projected, axis=1, keepdims=True)
-    weights = jnp.broadcast_to(weights.astype(jnp.bfloat16).astype(jnp.float32), (RECYCLED, LANES))
+    weights = jnp.broadcast_to(weights.astype(jnp.bfloat16).astype(jnp.float32), (RECYCLED, 2 * LANES))
+    wide = (2 * TILE, 2 * TILE * RECYCLED)
+    index = lax.broadcasted_iota(jnp.int32, wide, 0)
+    slot = lax.broadcasted_iota(jnp.int32, wide, 1)
+    spread_weights = jnp.sum(jnp.where(slot // (2 * TILE) == index, weights, 0.0), axis=0, keepdims=True)
+    mixing = jnp.where(slot % (2 * TILE) == index, spread_weights, 0.0).astype(jnp.bfloat16)
     planes, rows, _ = direction.shape
     near = row < S
     for plane in range(planes):
@@ -522,11 +561,8 @@
                     if field in coefficients:
                         factor = jnp.concatenate([coefficients[field]] * 2, axis=0)
                         found[index] = found[index] + factor * values
-            correction = 0.0
-            for vector in range(RECYCLED):
-                correction = correction + weights[vector : vector + 1] * recycled[vector, plane, part].astype(
-                    jnp.float32
-                )
+            vectors = recycled[:, plane, part].reshape(RECYCLED * 2 * TILE, LANES)
+            correction = jnp.dot(mixing, vectors, preferred_element_type=jnp.float32)
             delta_out[plane, part] = found[0]
             residual_out[plane, part] = found[1]
             direction_out[plane, part] = found[2] - correction
@@ -629,15 +665,22 @@
         weights_and_left(rows) + [pltpu.SemaphoreType.DMA],
         in_hbm=(recycled_images,),
     )
+    tall = [pltpu.VMEM((S, wide, TILE, LANES), jnp.float32), pltpu.VMEM((S - 1, wide, TILE, LANES), jnp.float32)]
+    cap_shape = (BASIS - 2, planes, TILE, LANES)
+    (cap,) = call(
+        first_cap_kernel,
+        [cap_shape],
+        (parity, *fields, low, high, whole_rims, first, shifts, rim_shifts, *levels),
+        tall + weights_and_left(TILE),
+    )
     caps, parts = call(
         caps_kernel,
-        [(BASIS - 2, planes, TILE, LANES), (devices, 2, LANES)],
-        (parity, *fields, low, high, whole_rims, first, second, images)
+        [cap_shape, (2 * devices, LANES)],
+        (parity, *fields, low, high, whole_rims, second, cap, images)
         + (shifts, rim_shifts, groups, sums, total, *levels),
-        [pltpu.VMEM((S, wide, block, LANES), jnp.float32), pltpu.VMEM((S - 1, wide, block, LANES), jnp.float32)]
-        + weights_and_left(block),
-    )
-    parts = lax.all_to_all(parts, AXES, 0, 0)
+        tall + weights_and_left(TILE),
+    )
+    parts = lax.all_to_all(parts, AXES, 0, 0, tiled=True)
     return call(finish_kernel, [shape] * 3, (parts, coupling, fields[0], fields[1], basis, caps, recycled))
 
 

time: 32.6 us -> 32.2 us (0.988)
  waiting for transfers between devices: 2.23 us -> 1.6 us
  Pallas kernels: 7.25 us -> 7.64 us
    ppermute x7, waiting for transfers between devices: 2.23 us -> 1.6 us  [moved(): return lax.ppermute(values, axes, pairs)]
    pallas_call x6 -> x7, Pallas kernels: 7.25 us -> 7.64 us  [call(): pl.pallas_call(kernel, out_shape=tuple(out_shape), in_specs=[in_smem if o...]
  transfers between devices with their start and end apart: 7 -> 7, of which waited for: 3 -> 2; matrix products, arithmetic and copies ran while one was open for 0% -> 0% of each run, Pallas kernels for 10% -> 12%
where the time goes in v3:
time: 32.2 us; the launch traced here: 32 us
  starting transfers between devices  11.6 us (36%)
  blocking collectives  10.3 us (32%)
  Pallas kernels  7.64 us (24%)
  waiting for transfers between devices  1.6 us (5%)
  between operations  0.7 us (2%)
    ppermute x7, starting transfers between devices, moved(): return lax.ppermute(values, axes, pairs)  11.6 us
    all_to_all x1, blocking collectives, body(): parts = lax.all_to_all(parts, AXES, 0, 0, tiled=True)  10.3 us
    pallas_call x7, Pallas kernels, call(): pl.pallas_call(kernel, out_shape=tuple(out_shape), in_specs=[in_smem if o...  7.64 us
    ppermute x7, waiting for transfers between devices, moved(): return lax.ppermute(values, axes, pairs)  1.6 us
  transfers between devices with their start and end apart: 7, of which 2 were waited for; matrix products, arithmetic and copies ran while one was open for 0% of the time, Pallas kernels for 12%

profile of v3, /device:TPU:0, one launch (start us, length us, event | category | flops | bytes accessed | tf_op | source)
XLA Modules:
  0.0 32.0 jit_solution(9554672271513470373)
XLA Ops:
  0.6 1.1 %shard_map.112 = (f32[8,32,128]{2,1,0:T(8,128)S(1)}, f32[8,32,128]{2,1,0:T(8,128)S(1)}, f32[8,32,128]{2,1,0:T(8,128)S(1)}, f32[10,32,128]{2,1,0:T(8,128)S(1)}, f...) custom-call(f32[8,32,128]{2,1,0:T(8,128)} %direction_in.1, f32[8,32,128]{2,1,0:T(8,128)} %residual_in.1, ...), custom_call_target="tpu_custom_call" | custom-call | tf_op jit(solution)/shard_map/pallas_call | solution.py:600
  1.7 0.5 %collective-permute-start = (f32[10,32,128]{2,1,0:T(8,128)S(1)}, f32[10,32,128]{2,1,0:T(8,128)S(1)}, u32[]{:S(2)}, u32[]{:S(2)}) collective-permute-start(f32[10,32,128]{2,1,0:T(8,128)S(1)} %get-tuple-element.29), channel_id=1, source_target_pairs={{0,8},{8,16},{16,24},{24,0},{1,9},{9,17},{17,25},{25,1},{2,10},{10... | collective-permute-start | bytes 491528 | tf_op jit(solution)/shard_map/ppermute | solution.py:591
  2.3 2.0 %collective-permute-start.1 = (f32[10,32,128]{2,1,0:T(8,128)S(1)}, f32[10,32,128]{2,1,0:T(8,128)S(1)}, u32[]{:S(2)}, u32[]{:S(2)}) collective-permute-start(f32[10,32,128]{2,1,0:T(8,128)S(1)} %get-tuple-element.30), channel_id=1, source_target_pairs={{0,24},{8,0},{16,8},{24,16},{1,25},{9,1},{17,9},{25,17},{2,26},{10... | collective-permute-start | bytes 491528 | tf_op jit(solution)/shard_map/ppermute | solution.py:591
  4.3 0.3 shard_map.113
  4.5 2.3 %collective-permute-start.2 = (f32[3,32,128]{2,1,0:T(8,128)S(1)}, f32[3,32,128]{2,1,0:T(8,128)S(1)}, u32[]{:S(2)}, u32[]{:S(2)}) collective-permute-start(f32[3,32,128]{2,1,0:T(8,128)S(1)} %get-tuple-element.32), channel_id=1, source_target_pairs={{0,1},{1,0},{2,3},{3,2},{4,5},{5,4},{6,7},{7,6},{8,9},{9,8},{10,11... | collective-permute-start | bytes 147464 | tf_op jit(solution)/shard_map/ppermute | solution.py:591
  6.8 0.0 collective-permute-start.3
  6.8 0.0 copy-start
  6.8 0.0 copy-start.2
  6.8 2.7 %collective-permute-start.4 = (f32[32,128]{1,0:T(8,128)S(1)}, f32[32,128]{1,0:T(8,128)S(1)}, u32[]{:S(2)}, u32[]{:S(2)}) collective-permute-start(f32[32,128]{1,0:T(8,128)S(1)} %get-tuple-element.34), channel_id=1, source_target_pairs={{0,9},{1,8},{8,1},{9,0},{16,25},{17,24},{24,17},{25,16},{2,11},{3,... | collective-permute-start | bytes 49160 | tf_op jit(solution)/shard_map/ppermute | solution.py:591
  9.5 1.4 %collective-permute-done.3.outward_next.outward_before = f32[32,128]{1,0:T(8,128)S(1)} collective-permute-done((f32[32,128]{1,0:T(8,128)S(1)}, f32[32,128]{1,0:T(8,128)S(1)}, u32[]{:S(2)}, u32[]{:S(2)}) %collective-permute-start.3) | collective-permute-done | bytes 16416 | tf_op jit(solution)/shard_map/ppermute | solution.py:591
  10.9 0.2 collective-permute-done.4.inward_next.inward_before
  11.1 0.0 collective-permute-done.2.rim_next.rim_before
  11.1 0.0 collective-permute-done.low
  11.1 0.0 collective-permute-done.1.high
  11.1 0.1 shard_map.114
  11.2 1.6 %collective-permute-start.6 = (f32[14,8,128]{2,1,0:T(8,128)S(1)}, f32[14,8,128]{2,1,0:T(8,128)S(1)}, u32[]{:S(2)}, u32[]{:S(2)}) collective-permute-start(f32[14,8,128]{2,1,0:T(8,128)S(1)} %get-tuple-element.37), channel_id=1, source_target_pairs={{0,2},{2,0},{4,6},{6,4},{1,3},{3,1},{5,7},{7,5},{8,10},{10,8},{12,... | collective-permute-start | bytes 172040 | tf_op jit(solution)/shard_map/ppermute | solution.py:591
  12.9 2.5 %collective-permute-start.5 = (f32[14,8,128]{2,1,0:T(8,128)S(1)}, f32[14,8,128]{2,1,0:T(8,128)S(1)}, u32[]{:S(2)}, u32[]{:S(2)}) collective-permute-start(f32[14,8,128]{2,1,0:T(8,128)S(1)} %get-tuple-element.36), channel_id=1, source_target_pairs={{0,6},{2,4},{4,2},{6,0},{1,7},{3,5},{5,3},{7,1},{8,14},{10,12},{12... | collective-permute-start | bytes 172040 | tf_op jit(solution)/shard_map/ppermute | solution.py:591
  15.3 0.0 copy-done
  15.4 0.0 copy-done.2
  15.4 2.9 %shard_map.115 = (f32[7,8,32,128]{3,2,1,0:T(8,128)S(1)}, f32[24,8,128]{2,1,0:T(8,128)S(1)}, f32[144,256]{1,0:T(8,128)S(1)}, f32[4,16,32,128]{3,2,1,0:T(8,128)S(1...) custom-call(f32[8,32,128]{2,1,0:T(8,128)S(1)} %get-tuple-element.26., ...), custom_call_target="tpu_custom_call" | custom-call | tf_op jit(solution)/shard_map/pallas_call | solution.py:600
  18.3 0.0 collective-permute-done.6.first
  18.3 0.0 copy-start.3
  18.3 0.7 %shard_map.116.cap = f32[7,8,8,128]{3,2,1,0:T(8,128)S(1)} custom-call(s32[1]{0:T(128)} %bitcast.parity, f32[8,32,128]{2,1,0:T(8,128)S(1)} %get-tuple-element.26.direction, f32[8,32,128]{2,1,0:T(8,128)S(1)} %get-tuple-element.27.residual, f32[8,32,128]{2,1,0:T(8,128)S(1)} %get-tuple-element.28.diagonal, f32[10,32,128]{2,1,0:T(8,128)S(1)} %collective-permute-done.low, ...), custom_call_target="tpu_custom_call" | custom-call | tf_op jit(solution)/shard_map/pallas_call | solution.py:600
  19.1 0.0 collective-permute-done.5.second
  19.1 0.2 copy-done.3
  19.2 0.0 copy-start.1
  19.3 1.2 %shard_map.117 = (f32[7,8,8,128]{3,2,1,0:T(8,128)S(1)}, f32[64,128]{1,0:T(8,128)S(1)}) custom-call(s32[1]{0:T(128)} %bitcast.parity, f32[8,32,128]{2,1,0:T(8,128)S(1)} %get-tuple-element.26.direction, f32[8,32,128]{2,1,0:T(8,128)S(1)} %get-tuple-element.27.residual, f32[8,32,128]{2,1,0:T(8,128)S(1)} %get-tuple-element.28.diagonal, ...), custom_call_target="tpu_custom_call" | custom-call | tf_op jit(solution)/shard_map/pallas_call | solution.py:600
  20.5 10.3 %all_to_all.11 = f32[32,2,128]{2,1,0:T(2,128)S(1)} all-to-all(f32[32,2,128]{2,1,0:T(2,128)S(1)} %bitcast.4), channel_id=1, replica_groups=mesh['gx'=4,'gy'=4,'gz'=2] {'gx','gy','gz'}, dimensions={0} | all-to-all | bytes 65536 | tf_op jit(solution)/shard_map/all_to_all | solution.py:683
  30.7 0.0 copy-done.1
  30.7 1.3 %shard_map.118 = (f32[8,32,128]{2,1,0:T(8,128)}, f32[8,32,128]{2,1,0:T(8,128)}, f32[8,32,128]{2,1,0:T(8,128)}) custom-call(f32[64,128]{1,0:T(8,128)S(1)} %bitcast.3, f32[16,128]{1,0:T(8,128)S(1)} %get-tuple-element.46.coupling, f32[8,32,128]{2,1,0:T(8,128)S(1)} %get-tuple-element.26.direction, f32[8,32,128]{2,1,0:T(8,128)S(1)} %get-tuple-element.27.residual, ...), custom_call_target="tpu_custom_call" | custom-call | tf_op jit(solution)/shard_map/pallas_call | solution.py:600
Async XLA Ops:
  1.7 9.4 %collective-permute-start = (f32[10,32,128]{2,1,0:T(8,128)S(1)}, f32[10,32,128]{2,1,0:T(8,128)S(1)}, u32[]{:S(2)}, u32[]{:S(2)}) collective-permute-start(f32[10,32,128]{2,1,0:T(8,128)S(1)} %get-tuple-element.29), channel_id=1, source_target_pairs={{0,8},{8,16},{16,24},{24,0},{1,9},{9,17},{17,25},{25,1},{2,10},{10... | collective-permute-start | bytes 491528 | tf_op jit(solution)/shard_map/ppermute | solution.py:591
  2.3 8.9 %collective-permute-start.1 = (f32[10,32,128]{2,1,0:T(8,128)S(1)}, f32[10,32,128]{2,1,0:T(8,128)S(1)}, u32[]{:S(2)}, u32[]{:S(2)}) collective-permute-start(f32[10,32,128]{2,1,0:T(8,128)S(1)} %get-tuple-element.30), channel_id=1, source_target_pairs={{0,24},{8,0},{16,8},{24,16},{1,25},{9,1},{17,9},{25,17},{2,26},{10... | collective-permute-start | bytes 491528 | tf_op jit(solution)/shard_map/ppermute | solution.py:591
  4.5 6.6 %collective-permute-start.2 = (f32[3,32,128]{2,1,0:T(8,128)S(1)}, f32[3,32,128]{2,1,0:T(8,128)S(1)}, u32[]{:S(2)}, u32[]{:S(2)}) collective-permute-start(f32[3,32,128]{2,1,0:T(8,128)S(1)} %get-tuple-element.32), channel_id=1, source_target_pairs={{0,1},{1,0},{2,3},{3,2},{4,5},{5,4},{6,7},{7,6},{8,9},{9,8},{10,11... | collective-permute-start | bytes 147464 | tf_op jit(solution)/shard_map/ppermute | solution.py:591
  6.8 4.1 %collective-permute-start.3 = (f32[32,128]{1,0:T(8,128)S(1)}, f32[32,128]{1,0:T(8,128)S(1)}, u32[]{:S(2)}, u32[]{:S(2)}) collective-permute-start(f32[32,128]{1,0:T(8,128)S(1)} %get-tuple-element.33), channel_id=1, source_target_pairs={{0,25},{1,24},{8,17},{9,16},{16,9},{17,8},{24,1},{25,0},{2,27},{3,... | collective-permute-start | bytes 49160 | tf_op jit(solution)/shard_map/ppermute | solution.py:591
  6.8 8.5 %copy-start = (bf16[512,256]{1,0:T(8,128)(2,1)S(1)}, bf16[512,256]{1,0:T(8,128)(2,1)}, u32[]{:S(2)}) copy-start(bf16[512,256]{1,0:T(8,128)(2,1)} %constant.19.clone.shifts) | copy-start | bytes 786436
  6.8 8.5 %copy-start.2 = (bf16[256,128]{1,0:T(8,128)(2,1)S(1)}, bf16[256,128]{1,0:T(8,128)(2,1)}, u32[]{:S(2)}) copy-start(bf16[256,128]{1,0:T(8,128)(2,1)} %constant.20.clone.rim_shifts) | copy-start | bytes 196612
  6.8 4.3 %collective-permute-start.4 = (f32[32,128]{1,0:T(8,128)S(1)}, f32[32,128]{1,0:T(8,128)S(1)}, u32[]{:S(2)}, u32[]{:S(2)}) collective-permute-start(f32[32,128]{1,0:T(8,128)S(1)} %get-tuple-element.34), channel_id=1, source_target_pairs={{0,9},{1,8},{8,1},{9,0},{16,25},{17,24},{24,17},{25,16},{2,11},{3,... | collective-permute-start | bytes 49160 | tf_op jit(solution)/shard_map/ppermute | solution.py:591
  11.2 7.1 %collective-permute-start.6 = (f32[14,8,128]{2,1,0:T(8,128)S(1)}, f32[14,8,128]{2,1,0:T(8,128)S(1)}, u32[]{:S(2)}, u32[]{:S(2)}) collective-permute-start(f32[14,8,128]{2,1,0:T(8,128)S(1)} %get-tuple-element.37), channel_id=1, source_target_pairs={{0,2},{2,0},{4,6},{6,4},{1,3},{3,1},{5,7},{7,5},{8,10},{10,8},{12,... | collective-permute-start | bytes 172040 | tf_op jit(solution)/shard_map/ppermute | solution.py:591
  12.9 6.2 %collective-permute-start.5 = (f32[14,8,128]{2,1,0:T(8,128)S(1)}, f32[14,8,128]{2,1,0:T(8,128)S(1)}, u32[]{:S(2)}, u32[]{:S(2)}) collective-permute-start(f32[14,8,128]{2,1,0:T(8,128)S(1)} %get-tuple-element.36), channel_id=1, source_target_pairs={{0,6},{2,4},{4,2},{6,0},{1,7},{3,5},{5,3},{7,1},{8,14},{10,12},{12... | collective-permute-start | bytes 172040 | tf_op jit(solution)/shard_map/ppermute | solution.py:591
  18.3 0.9 %copy-start.3 = (bf16[768,128]{1,0:T(8,128)(2,1)S(1)}, bf16[768,128]{1,0:T(8,128)(2,1)}, u32[]{:S(2)}) copy-start(bf16[768,128]{1,0:T(8,128)(2,1)} %constant.21.clone.groups) | copy-start | bytes 589828
  19.2 11.5 %copy-start.1 = (bf16[16,8,32,128]{3,2,1,0:T(8,128)(2,1)S(1)}, bf16[16,8,32,128]{3,2,1,0:T(8,128)(2,1)}, u32[]{:S(2)}) copy-start(bf16[16,8,32,128]{3,2,1,0:T(8,128)(2,1)} %recycled.1) | copy-start | bytes 3145732

commit v4 on v3

--- a/solution.py
+++ b/solution.py
@@ -360,8 +360,15 @@
 
 
 def first_cap_kernel(
-    parity, direction, residual, diagonal, low, high, rims, first, shifts, rim_shifts, inner_walk, inner_trail, inner_rim_walk, inner_rim_trail, cap_out, walk, trail, weight, left
+    parity, direction, residual, diagonal, low, high, rims, first, images, shifts, rim_shifts, inner_walk, inner_trail, inner_rim_walk, inner_rim_trail, cap_out, images_out, walk, trail, weight, left
 ):
+    planes, rows, _ = direction.shape
+    half = 2 * TILE
+    upper = lax.broadcasted_iota(jnp.int32, (RECYCLED, half, LANES), 1) < TILE
+    for x in range(planes):
+        chosen = jnp.where(upper, images[:, x, :half], images[:, x, rows - half :])
+        images_out[x] = chosen.reshape(RECYCLED * half, LANES)
+
     def emit(index, x, values):
         cap_out[index, x] = values
 
@@ -393,7 +400,6 @@
             return jnp.where(near, values[:TILE], values[rows - TILE :])
         return caps_out[index - 1 if index <= S else index - 2, x]
 
-    upper = lax.broadcasted_iota(jnp.int32, (RECYCLED, 2 * TILE, LANES), 1) < TILE
     families = products()
     sums = {}
     half = 2 * TILE
@@ -411,8 +417,7 @@
                 piece for value in values for piece in (jnp.where(near, value, 0.0), jnp.where(near, 0.0, value))
             ]
             rounded.append(jnp.concatenate(pieces, axis=0).astype(jnp.bfloat16))
-            images_here = jnp.where(upper, images[:, x + k, :half], images[:, x + k, rows - half :])
-            against.append(images_here.reshape(RECYCLED * half, LANES))
+            against.append(images[x + k])
         total = total + lax.dot_general(
             jnp.concatenate(rounded, axis=1),
             jnp.concatenate(against, axis=1),
@@ -667,16 +672,16 @@
     )
     tall = [pltpu.VMEM((S, wide, TILE, LANES), jnp.float32), pltpu.VMEM((S - 1, wide, TILE, LANES), jnp.float32)]
     cap_shape = (BASIS - 2, planes, TILE, LANES)
-    (cap,) = call(
+    cap, chosen = call(
         first_cap_kernel,
-        [cap_shape],
-        (parity, *fields, low, high, whole_rims, first, shifts, rim_shifts, *levels),
+        [cap_shape, jax.ShapeDtypeStruct((planes, RECYCLED * block, LANES), images.dtype)],
+        (parity, *fields, low, high, whole_rims, first, images, shifts, rim_shifts, *levels),
         tall + weights_and_left(TILE),
     )
     caps, parts = call(
         caps_kernel,
         [cap_shape, (2 * devices, LANES)],
-        (parity, *fields, low, high, whole_rims, second, cap, images)
+        (parity, *fields, low, high, whole_rims, second, cap, chosen)
         + (shifts, rim_shifts, groups, sums, total, *levels),
         tall + weights_and_left(TILE),
     )

time: 32.2 us -> 32.2 us (level)
  transfers between devices with their start and end apart: 7 -> 7, of which waited for: 2 -> 2; matrix products, arithmetic and copies ran while one was open for 0% -> 0% of each run, Pallas kernels for 12% -> 13%
where the time goes in v4:
time: 32.2 us; the launch traced here: 32 us
  starting transfers between devices  11.6 us (36%)
  blocking collectives  10.3 us (32%)
  Pallas kernels  7.76 us (24%)
  waiting for transfers between devices  1.6 us (5%)
  between operations  0.7 us (2%)
    ppermute x7, starting transfers between devices, moved(): return lax.ppermute(values, axes, pairs)  11.6 us
    all_to_all x1, blocking collectives, body(): parts = lax.all_to_all(parts, AXES, 0, 0, tiled=True)  10.3 us
    pallas_call x7, Pallas kernels, call(): pl.pallas_call(kernel, out_shape=tuple(out_shape), in_specs=[in_smem if o...  7.76 us
    ppermute x7, waiting for transfers between devices, moved(): return lax.ppermute(values, axes, pairs)  1.6 us
  transfers between devices with their start and end apart: 7, of which 2 were waited for; matrix products, arithmetic and copies ran while one was open for 0% of the time, Pallas kernels for 13%

profile of v4, /device:TPU:0, one launch (start us, length us, event | category | flops | bytes accessed | tf_op | source)
XLA Modules:
  0.0 32.0 jit_solution(3384111434530785551)
XLA Ops:
  0.6 1.1 %shard_map.112 = (f32[8,32,128]{2,1,0:T(8,128)S(1)}, f32[8,32,128]{2,1,0:T(8,128)S(1)}, f32[8,32,128]{2,1,0:T(8,128)S(1)}, f32[10,32,128]{2,1,0:T(8,128)S(1)}, f...) custom-call(f32[8,32,128]{2,1,0:T(8,128)} %direction_in.1, f32[8,32,128]{2,1,0:T(8,128)} %residual_in.1, ...), custom_call_target="tpu_custom_call" | custom-call | tf_op jit(solution)/shard_map/pallas_call | solution.py:605
  1.7 0.5 %collective-permute-start = (f32[10,32,128]{2,1,0:T(8,128)S(1)}, f32[10,32,128]{2,1,0:T(8,128)S(1)}, u32[]{:S(2)}, u32[]{:S(2)}) collective-permute-start(f32[10,32,128]{2,1,0:T(8,128)S(1)} %get-tuple-element.31), channel_id=1, source_target_pairs={{0,8},{8,16},{16,24},{24,0},{1,9},{9,17},{17,25},{25,1},{2,10},{10... | collective-permute-start | bytes 491528 | tf_op jit(solution)/shard_map/ppermute | solution.py:596
  2.3 2.0 %collective-permute-start.1 = (f32[10,32,128]{2,1,0:T(8,128)S(1)}, f32[10,32,128]{2,1,0:T(8,128)S(1)}, u32[]{:S(2)}, u32[]{:S(2)}) collective-permute-start(f32[10,32,128]{2,1,0:T(8,128)S(1)} %get-tuple-element.32), channel_id=1, source_target_pairs={{0,24},{8,0},{16,8},{24,16},{1,25},{9,1},{17,9},{25,17},{2,26},{10... | collective-permute-start | bytes 491528 | tf_op jit(solution)/shard_map/ppermute | solution.py:596
  4.3 0.3 shard_map.113
  4.5 2.3 %collective-permute-start.2 = (f32[3,32,128]{2,1,0:T(8,128)S(1)}, f32[3,32,128]{2,1,0:T(8,128)S(1)}, u32[]{:S(2)}, u32[]{:S(2)}) collective-permute-start(f32[3,32,128]{2,1,0:T(8,128)S(1)} %get-tuple-element.34), channel_id=1, source_target_pairs={{0,1},{1,0},{2,3},{3,2},{4,5},{5,4},{6,7},{7,6},{8,9},{9,8},{10,11... | collective-permute-start | bytes 147464 | tf_op jit(solution)/shard_map/ppermute | solution.py:596
  6.8 0.0 collective-permute-start.3
  6.8 0.0 copy-start
  6.8 0.0 copy-start.2
  6.8 2.7 %collective-permute-start.4 = (f32[32,128]{1,0:T(8,128)S(1)}, f32[32,128]{1,0:T(8,128)S(1)}, u32[]{:S(2)}, u32[]{:S(2)}) collective-permute-start(f32[32,128]{1,0:T(8,128)S(1)} %get-tuple-element.36), channel_id=1, source_target_pairs={{0,9},{1,8},{8,1},{9,0},{16,25},{17,24},{24,17},{25,16},{2,11},{3,... | collective-permute-start | bytes 49160 | tf_op jit(solution)/shard_map/ppermute | solution.py:596
  9.5 1.4 %collective-permute-done.3.outward_next.outward_before = f32[32,128]{1,0:T(8,128)S(1)} collective-permute-done((f32[32,128]{1,0:T(8,128)S(1)}, f32[32,128]{1,0:T(8,128)S(1)}, u32[]{:S(2)}, u32[]{:S(2)}) %collective-permute-start.3) | collective-permute-done | bytes 16416 | tf_op jit(solution)/shard_map/ppermute | solution.py:596
  10.9 0.2 collective-permute-done.4.inward_next.inward_before
  11.1 0.0 collective-permute-done.2.rim_next.rim_before
  11.1 0.0 collective-permute-done.low
  11.1 0.0 collective-permute-done.1.high
  11.1 0.1 shard_map.114
  11.2 1.6 %collective-permute-start.6 = (f32[14,8,128]{2,1,0:T(8,128)S(1)}, f32[14,8,128]{2,1,0:T(8,128)S(1)}, u32[]{:S(2)}, u32[]{:S(2)}) collective-permute-start(f32[14,8,128]{2,1,0:T(8,128)S(1)} %get-tuple-element.39), channel_id=1, source_target_pairs={{0,2},{2,0},{4,6},{6,4},{1,3},{3,1},{5,7},{7,5},{8,10},{10,8},{12,... | collective-permute-start | bytes 172040 | tf_op jit(solution)/shard_map/ppermute | solution.py:596
  12.9 2.5 %collective-permute-start.5 = (f32[14,8,128]{2,1,0:T(8,128)S(1)}, f32[14,8,128]{2,1,0:T(8,128)S(1)}, u32[]{:S(2)}, u32[]{:S(2)}) collective-permute-start(f32[14,8,128]{2,1,0:T(8,128)S(1)} %get-tuple-element.38), channel_id=1, source_target_pairs={{0,6},{2,4},{4,2},{6,0},{1,7},{3,5},{5,3},{7,1},{8,14},{10,12},{12... | collective-permute-start | bytes 172040 | tf_op jit(solution)/shard_map/ppermute | solution.py:596
  15.3 0.0 copy-done
  15.4 0.0 copy-done.2
  15.4 2.9 %shard_map.115 = (f32[7,8,32,128]{3,2,1,0:T(8,128)S(1)}, f32[24,8,128]{2,1,0:T(8,128)S(1)}, f32[144,256]{1,0:T(8,128)S(1)}, f32[4,16,32,128]{3,2,1,0:T(8,128)S(1...) custom-call(f32[8,32,128]{2,1,0:T(8,128)S(1)} %get-tuple-element.28., ...), custom_call_target="tpu_custom_call" | custom-call | tf_op jit(solution)/shard_map/pallas_call | solution.py:605
  18.3 0.0 collective-permute-done.6.first
  18.3 0.0 copy-start.3
  18.3 0.9 %shard_map.116 = (f32[7,8,8,128]{3,2,1,0:T(8,128)S(1)}, bf16[8,256,128]{2,1,0:T(8,128)(2,1)S(1)}) custom-call(s32[1]{0:T(128)} %bitcast.parity, f32[8,32,128]{2,1,0:T(8,128)S(1)} %get-tuple-element.28.direction, f32[8,32,128]{2,1,0:T(8,128)S(1)} %get-tuple-element.29.residual, f32[8,32,128]{2,1,0:T(8,128)S(1)} %get-tuple-element.30.diagonal, ...), custom_call_target="tpu_custom_call" | custom-call | tf_op jit(solution)/shard_map/pallas_call | solution.py:605
  19.2 0.0 collective-permute-done.5.second
  19.2 0.0 copy-done.3
  19.2 0.0 copy-start.1
  19.3 1.2 %shard_map.117 = (f32[7,8,8,128]{3,2,1,0:T(8,128)S(1)}, f32[64,128]{1,0:T(8,128)S(1)}) custom-call(s32[1]{0:T(128)} %bitcast.parity, f32[8,32,128]{2,1,0:T(8,128)S(1)} %get-tuple-element.28.direction, f32[8,32,128]{2,1,0:T(8,128)S(1)} %get-tuple-element.29.residual, f32[8,32,128]{2,1,0:T(8,128)S(1)} %get-tuple-element.30.diagonal, ...), custom_call_target="tpu_custom_call" | custom-call | tf_op jit(solution)/shard_map/pallas_call | solution.py:605
  20.5 10.3 %all_to_all.11 = f32[32,2,128]{2,1,0:T(2,128)S(1)} all-to-all(f32[32,2,128]{2,1,0:T(2,128)S(1)} %bitcast.4), channel_id=1, replica_groups=mesh['gx'=4,'gy'=4,'gz'=2] {'gx','gy','gz'}, dimensions={0} | all-to-all | bytes 65536 | tf_op jit(solution)/shard_map/all_to_all | solution.py:688
  30.7 0.0 copy-done.1
  30.7 1.3 %shard_map.118 = (f32[8,32,128]{2,1,0:T(8,128)}, f32[8,32,128]{2,1,0:T(8,128)}, f32[8,32,128]{2,1,0:T(8,128)}) custom-call(f32[64,128]{1,0:T(8,128)S(1)} %bitcast.3, f32[16,128]{1,0:T(8,128)S(1)} %get-tuple-element.50.coupling, f32[8,32,128]{2,1,0:T(8,128)S(1)} %get-tuple-element.28.direction, f32[8,32,128]{2,1,0:T(8,128)S(1)} %get-tuple-element.29.residual, ...), custom_call_target="tpu_custom_call" | custom-call | tf_op jit(solution)/shard_map/pallas_call | solution.py:605
Async XLA Ops:
  1.7 9.4 %collective-permute-start = (f32[10,32,128]{2,1,0:T(8,128)S(1)}, f32[10,32,128]{2,1,0:T(8,128)S(1)}, u32[]{:S(2)}, u32[]{:S(2)}) collective-permute-start(f32[10,32,128]{2,1,0:T(8,128)S(1)} %get-tuple-element.31), channel_id=1, source_target_pairs={{0,8},{8,16},{16,24},{24,0},{1,9},{9,17},{17,25},{25,1},{2,10},{10... | collective-permute-start | bytes 491528 | tf_op jit(solution)/shard_map/ppermute | solution.py:596
  2.3 8.9 %collective-permute-start.1 = (f32[10,32,128]{2,1,0:T(8,128)S(1)}, f32[10,32,128]{2,1,0:T(8,128)S(1)}, u32[]{:S(2)}, u32[]{:S(2)}) collective-permute-start(f32[10,32,128]{2,1,0:T(8,128)S(1)} %get-tuple-element.32), channel_id=1, source_target_pairs={{0,24},{8,0},{16,8},{24,16},{1,25},{9,1},{17,9},{25,17},{2,26},{10... | collective-permute-start | bytes 491528 | tf_op jit(solution)/shard_map/ppermute | solution.py:596
  4.5 6.6 %collective-permute-start.2 = (f32[3,32,128]{2,1,0:T(8,128)S(1)}, f32[3,32,128]{2,1,0:T(8,128)S(1)}, u32[]{:S(2)}, u32[]{:S(2)}) collective-permute-start(f32[3,32,128]{2,1,0:T(8,128)S(1)} %get-tuple-element.34), channel_id=1, source_target_pairs={{0,1},{1,0},{2,3},{3,2},{4,5},{5,4},{6,7},{7,6},{8,9},{9,8},{10,11... | collective-permute-start | bytes 147464 | tf_op jit(solution)/shard_map/ppermute | solution.py:596
  6.8 4.1 %collective-permute-start.3 = (f32[32,128]{1,0:T(8,128)S(1)}, f32[32,128]{1,0:T(8,128)S(1)}, u32[]{:S(2)}, u32[]{:S(2)}) collective-permute-start(f32[32,128]{1,0:T(8,128)S(1)} %get-tuple-element.35), channel_id=1, source_target_pairs={{0,25},{1,24},{8,17},{9,16},{16,9},{17,8},{24,1},{25,0},{2,27},{3,... | collective-permute-start | bytes 49160 | tf_op jit(solution)/shard_map/ppermute | solution.py:596
  6.8 8.5 %copy-start = (bf16[512,256]{1,0:T(8,128)(2,1)S(1)}, bf16[512,256]{1,0:T(8,128)(2,1)}, u32[]{:S(2)}) copy-start(bf16[512,256]{1,0:T(8,128)(2,1)} %constant.19.clone.shifts) | copy-start | bytes 786436
  6.8 8.5 %copy-start.2 = (bf16[256,128]{1,0:T(8,128)(2,1)S(1)}, bf16[256,128]{1,0:T(8,128)(2,1)}, u32[]{:S(2)}) copy-start(bf16[256,128]{1,0:T(8,128)(2,1)} %constant.20.clone.rim_shifts) | copy-start | bytes 196612
  6.8 4.3 %collective-permute-start.4 = (f32[32,128]{1,0:T(8,128)S(1)}, f32[32,128]{1,0:T(8,128)S(1)}, u32[]{:S(2)}, u32[]{:S(2)}) collective-permute-start(f32[32,128]{1,0:T(8,128)S(1)} %get-tuple-element.36), channel_id=1, source_target_pairs={{0,9},{1,8},{8,1},{9,0},{16,25},{17,24},{24,17},{25,16},{2,11},{3,... | collective-permute-start | bytes 49160 | tf_op jit(solution)/shard_map/ppermute | solution.py:596
  11.2 7.1 %collective-permute-start.6 = (f32[14,8,128]{2,1,0:T(8,128)S(1)}, f32[14,8,128]{2,1,0:T(8,128)S(1)}, u32[]{:S(2)}, u32[]{:S(2)}) collective-permute-start(f32[14,8,128]{2,1,0:T(8,128)S(1)} %get-tuple-element.39), channel_id=1, source_target_pairs={{0,2},{2,0},{4,6},{6,4},{1,3},{3,1},{5,7},{7,5},{8,10},{10,8},{12,... | collective-permute-start | bytes 172040 | tf_op jit(solution)/shard_map/ppermute | solution.py:596
  12.9 6.3 %collective-permute-start.5 = (f32[14,8,128]{2,1,0:T(8,128)S(1)}, f32[14,8,128]{2,1,0:T(8,128)S(1)}, u32[]{:S(2)}, u32[]{:S(2)}) collective-permute-start(f32[14,8,128]{2,1,0:T(8,128)S(1)} %get-tuple-element.38), channel_id=1, source_target_pairs={{0,6},{2,4},{4,2},{6,0},{1,7},{3,5},{5,3},{7,1},{8,14},{10,12},{12... | collective-permute-start | bytes 172040 | tf_op jit(solution)/shard_map/ppermute | solution.py:596
  18.3 0.9 %copy-start.3 = (bf16[768,128]{1,0:T(8,128)(2,1)S(1)}, bf16[768,128]{1,0:T(8,128)(2,1)}, u32[]{:S(2)}) copy-start(bf16[768,128]{1,0:T(8,128)(2,1)} %constant.21.clone.groups) | copy-start | bytes 589828
  19.2 11.5 %copy-start.1 = (bf16[16,8,32,128]{3,2,1,0:T(8,128)(2,1)S(1)}, bf16[16,8,32,128]{3,2,1,0:T(8,128)(2,1)}, u32[]{:S(2)}) copy-start(bf16[16,8,32,128]{3,2,1,0:T(8,128)(2,1)} %recycled.1) | copy-start | bytes 3145732
